TPU v7x, 256 devices: a whole 4x4x8 slice. The times are simulated.
256 devices in a mesh: tok: 32 (over x, z), feat: 8 (over y, core).
Axes of the slice: x: 4, y: 4, z: 8, core: 2. Of those that a mesh axis runs over, the one named last changes fastest.
Arguments:
- slab: bfloat16 [65536, 8192], P('tok', 'feat'), may hold values from -48 to 48
- sketch: bfloat16 [8192, 512], P('feat'), may hold values from -0.0625 to 0.0625
Outputs:
- q_basis: bfloat16 [65536, 512], P('tok')
- r_scaled: float32 [512, 512], replicated
- projected: float32 [8192, 512], P(('feat', 'tok'))
All inputs are finite; a program needn't handle non-finite values.
Results may differ from a plain program's by a relative error of at most 0.011.
Values may be sent and summed in bfloat16 or wider, within the bound.
No kernel may reach another device: no remote copies, remote signals or barrier semaphores. Data moves between devices by JAX's collectives and lax.ppermute only.
A program may use at most 64 MiB of HBM per device.

v0:
```python
import jax
import jax.numpy as jnp
from jax import lax
from jax.sharding import Mesh
from jax.sharding import PartitionSpec as P

FEAT = ("feat_0", "feat_1")
TOK = ("tok_0", "tok_1")
FEAT_TOK = ("feat_0", "feat_1", "tok_0", "tok_1")


HIGH = lax.Precision.HIGHEST


def in_blocks(array, dim, peers):
    before, after = (array.shape[:dim], array.shape[dim + 1 :])
    return jnp.moveaxis(array.reshape(*before, peers, -1, *after), dim, 0)


def summed_on_arrival(array, axis, dim):
    blocks = in_blocks(array, dim, lax.axis_size(axis))
    arrived = lax.all_to_all(blocks, axis, split_axis=0, concat_axis=0, tiled=True)
    return arrived.sum(axis=0)


def sum_in_two_steps(array, axes, dim):
    far, near = axes
    blocks = in_blocks(array, dim, lax.axis_size(far))
    nearer = summed_on_arrival(blocks, near, dim + 1)
    arrived = lax.all_to_all(nearer, far, split_axis=0, concat_axis=0, tiled=True)
    return arrived.sum(axis=0)


def rows_for(lines, peers):
    spare = -len(lines) % peers
    return jnp.pad(lines, [(0, spare)] + [(0, 0)] * (lines.ndim - 1))


def sent_to_all(array, axis):
    peers = lax.axis_size(axis)
    return lax.all_to_all(
        jnp.broadcast_to(array[None], (peers, *array.shape)), axis, 0, 0, tiled=True
    )


def joined_along(blocks, dim):
    blocks = jnp.moveaxis(blocks, 0, dim)
    shape = blocks.shape
    return blocks.reshape(*shape[:dim], shape[dim] * shape[dim + 1], *shape[dim + 2 :])


def gathered_by_axis(array, axes, dim):
    far, near = axes
    blocks = sent_to_all(sent_to_all(array, far), near)
    return joined_along(blocks.swapaxes(0, 1).reshape(-1, *array.shape), dim)


def total_of(array, axes):
    lines = array.reshape(-1, array.shape[-1])
    own = sum_in_two_steps(
        rows_for(lines, lax.axis_size(axes[0]) * lax.axis_size(axes[1])), axes, 0
    )
    whole = gathered_by_axis(own, axes, 0)
    return whole[: len(lines)].reshape(array.shape)


def sum_at_owner(array, axis, dim):
    peers = lax.axis_size(axis)
    blocks = lax.all_to_all(in_blocks(array, dim, peers), axis, 0, 0, tiled=True)
    return jnp.sum(blocks.astype(jnp.float32), axis=0)


def gram_of(rows):
    return lax.dot_general(
        rows, rows, (((0,), (0,)), ((), ())), precision=HIGH, preferred_element_type=jnp.float32
    )


def right_solve(lower, rows):
    return lax.linalg.triangular_solve(lower, rows, left_side=False, lower=True, transpose_a=True)


def body(slab, sketch):
    partial_rows = jnp.dot(slab, sketch, preferred_element_type=jnp.float32)
    sketched = sum_in_two_steps(partial_rows, ("feat_0", "feat_1"), 0)
    lower_one = jnp.linalg.cholesky(
        total_of(gram_of(sketched), (("tok_0", "tok_1"), ("feat_0", "feat_1")))
    )
    own_basis = right_solve(lower_one, sketched).astype(jnp.bfloat16)
    q_basis = gathered_by_axis(own_basis, ("feat_0", "feat_1"), 0)
    factor = lower_one.T
    token_count = slab.shape[0] * lax.axis_size(TOK)
    r_scaled = factor / jnp.sqrt(jnp.float32(token_count))
    projected = sum_at_owner(
        lax.dot_general(
            slab, q_basis, (((0,), (0,)), ((), ())), preferred_element_type=jnp.float32
        ).astype(jnp.bfloat16),
        TOK,
        0,
    )
    return (q_basis, r_scaled, projected)


def solution(mesh):
    split = Mesh(mesh.devices.reshape(4, 8, 4, 2), ("tok_0", "tok_1", "feat_0", "feat_1"))
    in_specs = (P(TOK, FEAT), P(FEAT, None))
    out_specs = (P(TOK, None), P(), P(FEAT_TOK, None))
    return jax.shard_map(body, mesh=split, in_specs=in_specs, out_specs=out_specs, check_vma=False)
```

profile of v0, /device:TPU:32, one launch (start us, length us, event | category | flops | bytes accessed | tf_op | source)
XLA Modules:
  0.0 343.3 jit_solution(11561899901245988015)
XLA Ops:
  1.9 4.5 %fusion.37 = f32[2048,512]{1,0:T(8,128)S(1)} fusion(bf16[2048,1024]{1,0:T(8,128)(2,1)} %param.2, bf16[1024,512]{1,0:T(8,128)(2,1)S(1)} %copy-done), kind=kOutput, calls=%fused_computation.79 | convolution fusion | flops 2147483648 | bytes 9437184 | tf_op jit(solution)/shard_map/dot_general | solution.py:84
  6.8 8.2 %all_to_all.45 = f32[2,4,256,512]{3,2,1,0:T(8,128)} all-to-all(f32[2,4,256,512]{3,2,1,0:T(8,128)S(1)} %bitcast.79), channel_id=1, replica_groups=mesh['tok_0'=4,'tok_1'=8,'feat_0'=4,'feat_1'=2] {'feat_1'}, dimensions={0} | all-to-all | bytes 8388608 | tf_op jit(solution)/shard_map/all_to_all | solution.py:22
  15.0 2.9 reduce_sum.45
  17.9 31.0 %all_to_all.46 = f32[4,256,512]{2,1,0:T(8,128)} all-to-all(f32[4,256,512]{2,1,0:T(8,128)S(1)} %reduce_sum.45), channel_id=1, replica_groups=mesh['tok_0'=4,'tok_1'=8,'feat_0'=4,'feat_1'=2] {'feat_0'}, dimensions={0} | all-to-all | bytes 4194304 | tf_op jit(solution)/shard_map/all_to_all | solution.py:30
  53.1 18.4 %all_to_all.47 = f32[8,32,2,512]{3,2,1,0:T(2,128)S(1)} all-to-all(f32[8,32,2,512]{3,2,1,0:T(2,128)S(1)} %copy.46), channel_id=1, replica_groups=mesh['tok_0'=4,'tok_1'=8,'feat_0'=4,'feat_1'=2] {'feat_0','feat_1'}, dimensions={0} | all-to-all | bytes 2097152 | tf_op jit(solution)/shard_map/all_to_all | solution.py:22
  72.0 20.6 %all_to_all.48 = f32[32,2,512]{2,1,0:T(2,128)S(1)} all-to-all(f32[32,2,512]{2,1,0:T(2,128)S(1)} %reduce_sum.47), channel_id=1, replica_groups=mesh['tok_0'=4,'tok_1'=8,'feat_0'=4,'feat_1'=2] {'tok_0','tok_1'}, dimensions={0} | all-to-all | bytes 262144 | tf_op jit(solution)/shard_map/all_to_all | solution.py:30
  92.7 13.9 %all_to_all.49 = f32[32,2,512]{2,1,0:T(2,128)S(1)} all-to-all(f32[32,2,512]{2,1,0:T(2,128)S(1)} %broadcast_in_dim.10), channel_id=1, replica_groups=mesh['tok_0'=4,'tok_1'=8,'feat_0'=4,'feat_1'=2] {'tok_0','tok_1'}, dimensions={0} | all-to-all | bytes 262144 | tf_op jit(solution)/shard_map/all_to_all | solution.py:41
  107.8 3.7 %all-to-all-start.5 = ((f32[8,32,2,512]{3,2,1,0:T(2,128)}), f32[8,32,2,512]{3,2,1,0:T(2,128)S(1)}, u32[]{:S(2)}, u32[]{:S(2)}) async-start(f32[8,32,2,512]{3,2,1,0:T(2,128)} %broadcast_in_dim.11), calls=%async_computation.5 | async-start | bytes 2097152 | tf_op jit(solution)/shard_map/all_to_all | solution.py:41
  111.6 15.7 %all-to-all-done.5 = f32[8,32,2,512]{3,2,1,0:T(2,128)S(1)} async-done(((f32[8,32,2,512]{3,2,1,0:T(2,128)}), f32[8,32,2,512]{3,2,1,0:T(2,128)S(1)}, u32[]{:S(2)}, u32[]{:S(2)}) %all-to-all-start.5) | async-done | bytes 1048608 | tf_op jit(solution)/shard_map/all_to_all | solution.py:41
  134.5 11.7 %cholesky.104 = f32[128,128]{1,0:T(8,128)S(1)} custom-call(f32[128,128]{1,0:T(8,128)S(1)} %cholesky.266), custom_call_target="Cholesky" | custom-call | tf_op jit(solution)/shard_map/jit(cholesky)/cholesky | solution.py:86
  146.4 9.8 %custom-call.30 = f32[1,128,128]{1,2,0:T(8,128)S(1)} custom-call(f32[1,128,128]{2,1,0:T(8,128)S(1)} %get-tuple-element.50), custom_call_target="InvertDiagBlocksLowerTriangular" | custom-call | tf_op jit(solution)/shard_map/jit(cholesky)/cholesky | solution.py:86
  158.7 11.7 %cholesky.217 = f32[128,128]{1,0:T(8,128)S(1)} custom-call(f32[128,128]{1,0:T(8,128)S(1)} %cholesky.270), custom_call_target="Cholesky" | custom-call | tf_op jit(solution)/shard_map/jit(cholesky)/cholesky | solution.py:86
  170.6 9.8 %custom-call.31 = f32[1,128,128]{1,2,0:T(8,128)S(1)} custom-call(f32[1,128,128]{2,1,0:T(8,128)S(1)} %get-tuple-element.47), custom_call_target="InvertDiagBlocksLowerTriangular" | custom-call | tf_op jit(solution)/shard_map/jit(cholesky)/cholesky | solution.py:86
  182.0 11.7 %cholesky.238 = f32[128,128]{1,0:T(8,128)S(1)} custom-call(f32[128,128]{1,0:T(8,128)S(1)} %cholesky.275), custom_call_target="Cholesky" | custom-call | tf_op jit(solution)/shard_map/jit(cholesky)/cholesky | solution.py:86
  194.5 9.8 %custom-call.32 = f32[1,128,128]{1,2,0:T(8,128)S(1)} custom-call(f32[1,128,128]{2,1,0:T(8,128)S(1)} %get-tuple-element.44), custom_call_target="InvertDiagBlocksLowerTriangular" | custom-call | tf_op jit(solution)/shard_map/jit(cholesky)/cholesky | solution.py:86
  205.8 11.9 %cholesky.255 = f32[128,128]{1,0:T(8,128)S(1)} custom-call(f32[128,128]{1,0:T(8,128)S(1)} %convolution_subtract_fusion.5), custom_call_target="Cholesky" | custom-call | tf_op jit(solution)/shard_map/jit(cholesky)/cholesky | solution.py:86
  223.1 11.7 %while.1 = (s32[]{:T(128)}, f32[512,512]{1,0:T(8,128)}, s32[4,2]{0,1:T(2,128)S(1)}, f32[4,128,128]{2,1,0:T(8,128)S(1)}, s32[]{:T(128)}) while((s32[]{:T(128)}, f32[512,512]{1,0:T(8,128)}, s32[4,2]{0,1:T(2,128)S(1)}, f32[4,128,128]{2,1,0:T(8,128)S(1)}, s32[]{:T(128)}) %tuple.41), condition=%wide.while_cond, body=%wide.while_body.sunk | while | flops 2 | bytes 131181 | solution.py:80
  229.7 2.2 bitcast_dynamic-update-slice_fusion.2
  234.9 39.3 %custom-call.33 = f32[4,128,128]{1,2,0:T(8,128)S(1)} custom-call(f32[4,128,128]{2,1,0:T(8,128)S(1)} %get-tuple-element.10), custom_call_target="InvertDiagBlocksLowerTriangular" | custom-call | tf_op jit(solution)/shard_map/triangular_solve | solution.py:80
  280.2 17.5 %all_to_all.50 = bf16[4,256,512]{2,1,0:T(8,128)(2,1)S(1)} all-to-all(bf16[4,256,512]{2,1,0:T(8,128)(2,1)S(1)} %broadcast_in_dim.12), channel_id=1, replica_groups=mesh['tok_0'=4,'tok_1'=8,'feat_0'=4,'feat_1'=2] {'feat_0'}, dimensions={0} | all-to-all | bytes 2097152 | tf_op jit(solution)/shard_map/all_to_all | solution.py:41
  298.0 5.7 %all_to_all.51 = bf16[2,4,256,512]{3,2,1,0:T(8,128)(2,1)S(1)} all-to-all(bf16[2,4,256,512]{3,2,1,0:T(8,128)(2,1)S(1)} %broadcast_in_dim.13), channel_id=1, replica_groups=mesh['tok_0'=4,'tok_1'=8,'feat_0'=4,'feat_1'=2] {'feat_1'}, dimensions={0} | all-to-all | bytes 4194304 | tf_op jit(solution)/shard_map/all_to_all | solution.py:41
  305.1 2.3 fusion
  308.8 4.6 %all-to-all-start.8 = ((bf16[32,32,512]{2,1,0:T(8,128)(2,1)}), bf16[32,32,512]{2,1,0:T(8,128)(2,1)S(1)}, u32[]{:S(2)}, u32[]{:S(2)}) async-start(bf16[32,32,512]{2,1,0:T(8,128)(2,1)} %bitcast.83), calls=%async_computation.8 | async-start | bytes 2097152 | tf_op jit(solution)/shard_map/all_to_all | solution.py:69
  314.7 27.4 %all-to-all-done.8 = bf16[32,32,512]{2,1,0:T(8,128)(2,1)S(1)} async-done(((bf16[32,32,512]{2,1,0:T(8,128)(2,1)}), bf16[32,32,512]{2,1,0:T(8,128)(2,1)S(1)}, u32[]{:S(2)}, u32[]{:S(2)}) %all-to-all-start.8) | async-done | bytes 1048608 | tf_op jit(solution)/shard_map/all_to_all | solution.py:69
  (71 shorter events, 44.6 us)
Async XLA Ops:
  0.6 1.2 copy-start
  107.8 19.4 %all-to-all-start.5 = ((f32[8,32,2,512]{3,2,1,0:T(2,128)}), f32[8,32,2,512]{3,2,1,0:T(2,128)S(1)}, u32[]{:S(2)}, u32[]{:S(2)}) async-start(f32[8,32,2,512]{3,2,1,0:T(2,128)} %broadcast_in_dim.11), calls=%async_computation.5 | async-start | bytes 2097152 | tf_op jit(solution)/shard_map/all_to_all | solution.py:41
  133.5 1.0 copy-start.2
  297.9 7.2 %copy-start.4 = (bf16[2048,1024]{1,0:T(8,128)(2,1)S(1)}, bf16[2048,1024]{1,0:T(8,128)(2,1)}, u32[]{:S(2)}) copy-start(bf16[2048,1024]{1,0:T(8,128)(2,1)} %param.2) | copy-start | bytes 12582916
  303.8 1.3 copy-start.3
  307.5 5.9 %copy-start.1 = (f32[512,512]{0,1:T(8,128)S(1)}, f32[512,512]{0,1:T(8,128)}, u32[]{:S(2)}) copy-start(f32[512,512]{0,1:T(8,128)} %get-tuple-element.39) | copy-start | bytes 3145732
  308.8 33.3 %all-to-all-start.8 = ((bf16[32,32,512]{2,1,0:T(8,128)(2,1)}), bf16[32,32,512]{2,1,0:T(8,128)(2,1)S(1)}, u32[]{:S(2)}, u32[]{:S(2)}) async-start(bf16[32,32,512]{2,1,0:T(8,128)(2,1)} %bitcast.83), calls=%async_computation.8 | async-start | bytes 2097152 | tf_op jit(solution)/shard_map/all_to_all | solution.py:69
where the time goes:
time: 350 us; the launch traced here: 343 us
  other arithmetic  127 us (36%)
  blocking collectives  115 us (33%)
  waiting for transfers between devices  43.1 us (12%)
  local copies, waits for them, and re-layouts  26.3 us (8%)
  matrix products  19.1 us (5%)
  starting transfers between devices  8.29 us (2%)
  between operations  4.17 us (1%)
    another operation x14, other arithmetic, body(): jnp.linalg.cholesky(total_of(gram_of(sketched), (('tok_0', 'tok_1'), ('fe...  78.6 us
    all_to_all x2, blocking collectives, sum_in_two_steps(): lax.all_to_all(nearer, far, split_axis=0, concat_axis=0, tiled=True)  51.7 us
    another operation x3, other arithmetic, right_solve(): lax.linalg.triangular_solve(lower, rows, left_side=False, lower=True, tra...  39.3 us
    all_to_all x3, blocking collectives, sent_to_all(): lax.all_to_all(jnp.broadcast_to(array[None], (peers, *array.shape)), axis...  37 us
    all_to_all x1, waiting for transfers between devices, sum_at_owner(): lax.all_to_all(in_blocks(array, dim, peers), axis, 0, 0, tiled=True)  27.4 us
    all_to_all x2, blocking collectives, summed_on_arrival(): lax.all_to_all(blocks, axis, split_axis=0, concat_axis=0, tiled=True)  26.6 us
    all_to_all x1, waiting for transfers between devices, sent_to_all(): lax.all_to_all(jnp.broadcast_to(array[None], (peers, *array.shape)), axis...  15.7 us
    another operation x12, local copies, waits for them, and re-layouts  11.6 us
  transfers between devices with their start and end apart: 2, of which 2 were waited for; matrix products, arithmetic and copies ran while one was open for 0% of the time, Pallas kernels for 0%

commit v1 on v0

v1 whole, which is shorter than its diff:
```python
import jax
import jax.numpy as jnp
from jax import lax
from jax.experimental import pallas as pl
from jax.experimental.pallas import tpu as pltpu
from jax.sharding import Mesh
from jax.sharding import PartitionSpec as P

HIGH = lax.Precision.HIGHEST
NB, PB = 128, 8

def diag_factor(block):
    sub = lax.broadcasted_iota(jnp.int32, (PB, NB), 0)
    lane = lax.broadcasted_iota(jnp.int32, (PB, NB), 1)
    n = NB // PB
    xs = [block[PB * p:PB * (p + 1), :] for p in range(n)]
    vs = [jnp.where(lane == sub + PB * p, 1.0, 0.0).astype(jnp.float32) for p in range(n)]
    rows, invs = [], []
    for p in range(n):
        x, v = xs[p], vs[p]
        cols = [jnp.broadcast_to(x[:, PB * p + k:PB * p + k + 1], (PB, NB)) for k in range(PB)]
        scale = jnp.ones((PB, NB), jnp.float32)
        for k in range(PB):
            r = lax.rsqrt(jnp.broadcast_to(cols[k][k:k + 1, :], (PB, NB)))
            scale = jnp.where(sub == k, r, scale)
            coef = jnp.where(sub > k, cols[k] * (r * r), 0.0)
            for j in range(k + 1, PB):
                cols[j] = cols[j] - coef * cols[j][k:k + 1, :]
            x = x - coef * x[k:k + 1, :]
            v = v - coef * v[k:k + 1, :]
        x, v = x * scale, v * scale
        rows.append(jnp.where(lane >= sub + PB * p, x, 0.0))
        invs.append(v)
        for q in range(p + 1, n):
            pick = lane == sub + PB * q
            for k in range(PB):
                row = jnp.broadcast_to(x[k:k + 1, :], (PB, NB))
                c = jnp.sum(jnp.where(pick, row, 0.0), axis=1, keepdims=True)
                xs[q] = xs[q] - c * row
                vs[q] = vs[q] - c * v[k:k + 1, :]
    return jnp.concatenate(rows, 0), jnp.concatenate(invs, 0)

def tn(a, b):
    return lax.dot_general(a, b, (((0,), (0,)), ((), ())), precision=HIGH, preferred_element_type=jnp.float32)

def nn(a, b):
    return jnp.dot(a, b, precision=HIGH, preferred_element_type=jnp.float32)

def factor_in_place(s_ref, r_ref, w_ref):
    n = s_ref.shape[0] // NB
    at = lambda i: slice(NB * i, NB * (i + 1))
    r_ref[...] = jnp.zeros_like(r_ref)
    w_ref[...] = jnp.zeros_like(w_ref)
    for b in range(n):
        upper, inv = diag_factor(s_ref[at(b), at(b)])
        r_ref[at(b), at(b)] = upper
        w_ref[at(b), at(b)] = inv
        if b:
            left = tn(r_ref[0:NB * b, at(b)], w_ref[0:NB * b, 0:NB * b])
            w_ref[at(b), 0:NB * b] = -nn(inv, left)
        if b < n - 1:
            rest = slice(NB * (b + 1), NB * n)
            r_ref[at(b), rest] = nn(inv, s_ref[at(b), rest])
            for j in range(b + 1, n):
                tail = slice(NB * j, NB * n)
                s_ref[at(j), tail] = s_ref[at(j), tail] - tn(r_ref[at(b), at(j)], r_ref[at(b), tail])

X, Z, Y, C = "tok_0", "tok_1", "feat_0", "feat_1"
TOK = (X, Z)
LEVEL = 14.0
TAIL = 8
F32, BF16, F16 = jnp.float32, jnp.bfloat16, jnp.float16
VMEM = pl.BlockSpec(memory_space=pltpu.VMEM)
SMEM = pl.BlockSpec(memory_space=pltpu.SMEM)


def struct(shape, dtype):
    return jax.ShapeDtypeStruct(shape, dtype)


def exchange(blocks, axis):
    return lax.all_to_all(blocks, axis, 0, 0, tiled=True)


def sent_to_all(array, axis):
    peers = lax.axis_size(axis)
    return exchange(jnp.broadcast_to(array[None], (peers, *array.shape)), axis)


def from_partner(array):
    return lax.ppermute(array, C, [(0, 1), (1, 0)])


def packed(values):
    power = jnp.clip(jnp.floor(jnp.log2(jnp.max(jnp.abs(values)))), -100.0, 40.0)
    tail = jnp.full((*values.shape[:-2], TAIL, values.shape[-1]), power.astype(F16))
    return jnp.concatenate([(values * jnp.exp2(LEVEL - power)).astype(F16), tail], axis=-2)


def unpacked(blocks):
    rows = blocks.shape[1] - TAIL
    power = blocks[:, rows : rows + 1, :1].astype(F32)
    return blocks[:, :rows, :].astype(F32) * jnp.exp2(power - LEVEL)


def split(blocks):
    values = unpacked(blocks).reshape(-1, blocks.shape[-1])
    high = lax.reduce_precision(values, 8, 7)
    return high.astype(BF16), (values - high).astype(BF16)


def dot_tn(a, b):
    return lax.dot_general(a, b, (((0,), (0,)), ((), ())), preferred_element_type=F32)


def dot_nt(a, b):
    return lax.dot_general(a, b, (((1,), (1,)), ((), ())), preferred_element_type=F32)


def share_kernel(place_ref, high_ref, low_ref, share_ref):
    strip = share_ref.shape[0]
    at = pl.ds(pl.multiple_of(place_ref[1] * strip, strip), strip)
    high, low = high_ref[...], low_ref[...]
    share_ref[...] = dot_tn(high_ref[:, at], high) + (
        dot_tn(high_ref[:, at], low) + dot_tn(low_ref[:, at], high)
    )


def basis_kernel(
    place_ref, mine_ref, other_ref, hm_ref, lm_ref, ho_ref, lo_ref, q_ref, r_ref, w_ref, s_ref, wh_ref, wl_ref
):
    core = place_ref[0]
    blocks, half, columns = mine_ref.shape
    for i in range(blocks):
        s_ref[pl.ds(pl.multiple_of(2 * half * i + half * core, half), half), :] = mine_ref[i]
        s_ref[pl.ds(pl.multiple_of(2 * half * i + half * (1 - core), half), half), :] = other_ref[i]
    factor_in_place(s_ref, r_ref, w_ref)
    inverse = w_ref[...]
    high = inverse.astype(BF16)
    wh_ref[...] = high
    wl_ref[...] = (inverse - high.astype(F32)).astype(BF16)
    rows = hm_ref.shape[0]
    step = 256
    for place, h_ref, l_ref in ((core, hm_ref, lm_ref), (1 - core, ho_ref, lo_ref)):
        def some_rows(i, _, place=place, h_ref=h_ref, l_ref=l_ref):
            at = pl.ds(pl.multiple_of(i * step, step), step)
            out = pl.ds(pl.multiple_of(place * rows + i * step, step), step)
            for j in range(0, columns, 256):
                k = j + 256
                wh, wl = wh_ref[j:k, :k], wl_ref[j:k, :k]
                h = h_ref[at, :k]
                q_ref[out, j:k] = (
                    dot_nt(h, wh) + (dot_nt(h, wl) + dot_nt(l_ref[at, :k], wh))
                ).astype(BF16)
            return 0
        lax.fori_loop(0, rows // step, some_rows, 0)


def body(slab, sketch):
    core, row = lax.axis_index(C), lax.axis_index(Y)
    place = jnp.stack([core, row]).astype(jnp.int32)
    tokens, columns = slab.shape[0], sketch.shape[1]
    half, block, strip = tokens // 2, tokens // 8, columns // 4
    halves = slab.reshape(2, half, slab.shape[1])

    def half_rows(which):
        return lax.dynamic_index_in_dim(halves, which, 0, keepdims=False)

    def partial(which):
        return jnp.dot(half_rows(which), sketch, preferred_element_type=F32)

    theirs = from_partner(partial(1 - core))
    pair_sum = (partial(core) + theirs).reshape(4, block, columns)
    own = unpacked(exchange(packed(pair_sum), Y)).sum(axis=0)
    mine = sent_to_all(packed(own), Y)
    other = from_partner(mine)
    high_mine, low_mine = split(mine)
    share = pl.pallas_call(
        share_kernel,
        out_shape=struct((strip, columns), F32),
        in_specs=[SMEM, VMEM, VMEM],
        out_specs=VMEM,
        name="share",
    )(place, high_mine, low_mine)
    high_other, low_other = split(other)

    shares = share.reshape(2, strip // 2, columns)
    kept = lax.dynamic_index_in_dim(shares, core, 0, keepdims=False)
    given = lax.dynamic_index_in_dim(shares, 1 - core, 0, keepdims=False)
    strip_sum = kept + from_partner(given)
    total = exchange(strip_sum.reshape(32, -1, columns), TOK).sum(axis=0)
    done = sent_to_all(total, TOK).reshape(strip // 2, columns)

    def onto(which, values):
        return lax.dot_general(
            half_rows(which), values, (((0,), (0,)), ((), ())), preferred_element_type=F32
        )

    images = onto(core, high_mine) + onto(core, low_mine)
    images = images + (onto(1 - core, high_other) + onto(1 - core, low_other))
    image = exchange(images.astype(BF16).reshape(32, -1, columns), TOK)

    strips = sent_to_all(done, Y)
    square = struct((columns, columns), F32)
    q_basis, upper, inverse = pl.pallas_call(
        basis_kernel,
        out_shape=(struct((tokens, columns), BF16), square, square),
        in_specs=[SMEM] + [VMEM] * 6,
        out_specs=(VMEM,) * 3,
        scratch_shapes=[
            pltpu.VMEM((columns, columns), F32),
            pltpu.VMEM((columns, columns), BF16),
            pltpu.VMEM((columns, columns), BF16),
        ],
        name="basis",
    )(place, strips, from_partner(strips), high_mine, low_mine, high_other, low_other)
    token_count = tokens * lax.axis_size(TOK)
    r_scaled = upper / jnp.sqrt(jnp.float32(token_count))
    projected = lax.dot_general(
        image.astype(F32).sum(axis=0), inverse, (((1,), (1,)), ((), ())), precision=HIGH,
        preferred_element_type=F32,
    )
    return (q_basis, r_scaled, projected)


def solution(mesh):
    split_mesh = Mesh(mesh.devices.reshape(4, 8, 4, 2), (X, Z, Y, C))
    in_specs = (P(TOK, (Y, C)), P((Y, C), None))
    out_specs = (P(TOK, None), P(), P((Y, C, X, Z), None))
    return jax.shard_map(body, mesh=split_mesh, in_specs=in_specs, out_specs=out_specs, check_vma=False)
```

time: 350 us -> 162 us (0.46); the launches traced: 343 us -> 159 us
  other arithmetic: 127 us -> 14.5 us
  blocking collectives: 115 us -> 20 us
  Pallas kernels: 0 us -> 33.2 us
  starting transfers between devices: 8.29 us -> 29.3 us
  local copies, waits for them, and re-layouts: 26.3 us -> 7.33 us
  waiting for transfers between devices: 43.1 us -> 31.8 us
    another operation x17 -> x1, other arithmetic: 118 us -> 0.59 us  [body(): place = jnp.stack([core, row]).astype(jnp.int32)]
    all_to_all x7 -> x1, blocking collectives: 115 us -> 20 us  [exchange(): return lax.all_to_all(blocks, axis, 0, 0, tiled=True)]
    pallas_call x0 -> x2, Pallas kernels: none -> 33.2 us  [the longest x1 30.3 us: body(): pl.pallas_call(basis_kernel, out_shape=(struct((tokens, columns), BF16),...]
    all_to_all x2 -> x5, starting transfers between devices: 8.29 us -> 28.5 us  [exchange(): return lax.all_to_all(blocks, axis, 0, 0, tiled=True)]
    all_to_all x2 -> x5, waiting for transfers between devices: 43.1 us -> 25.5 us  [exchange(): return lax.all_to_all(blocks, axis, 0, 0, tiled=True)]
    another operation x21 -> x0, local copies, waits for them, and re-layouts: 15.6 us -> none
    dot_general x3 -> x7, matrix products: 7.88 us -> 20.9 us  [the longest x4 12.3 us: onto(): lax.dot_general(half_rows(which), values, (((0,), (0,)), ((), ())), prefe...]
    another operation x13 -> x0, matrix products: 11.2 us -> none  [the longest x7 5.76 us: right_solve(): lax.linalg.triangular_solve(lower, rows, left_side=False, lower=True, tra...]
  transfers between devices with their start and end apart: 2 -> 9, of which waited for: 2 -> 7; matrix products, arithmetic and copies ran while one was open for 0% -> 15% of each run, Pallas kernels for 0% -> 19%
where the time goes in v1:
time: 162 us; the launch traced here: 159 us
  Pallas kernels  33.2 us (20%)
  waiting for transfers between devices  31.8 us (20%)
  starting transfers between devices  29.3 us (18%)
  matrix products  20.9 us (13%)
  blocking collectives  20 us (12%)
  other arithmetic  14.5 us (9%)
  local copies, waits for them, and re-layouts  7.33 us (5%)
  between operations  2.28 us (1%)
    pallas_call x1, Pallas kernels, body(): pl.pallas_call(basis_kernel, out_shape=(struct((tokens, columns), BF16),...  30.3 us
    all_to_all x5, starting transfers between devices, exchange(): return lax.all_to_all(blocks, axis, 0, 0, tiled=True)  28.5 us
    all_to_all x5, waiting for transfers between devices, exchange(): return lax.all_to_all(blocks, axis, 0, 0, tiled=True)  25.5 us
    all_to_all x1, blocking collectives, exchange(): return lax.all_to_all(blocks, axis, 0, 0, tiled=True)  20 us
    dot_general x4, matrix products, onto(): lax.dot_general(half_rows(which), values, (((0,), (0,)), ((), ())), prefe...  12.3 us
    dot_general x2, matrix products, partial(): return jnp.dot(half_rows(which), sketch, preferred_element_type=F32)  6.97 us
    convert_element_type x4, other arithmetic, split(): return (high.astype(BF16), (values - high).astype(BF16))  6.8 us
    ppermute x4, waiting for transfers between devices, from_partner(): return lax.ppermute(array, C, [(0, 1), (1, 0)])  6.26 us
  transfers between devices with their start and end apart: 9, of which 7 were waited for; matrix products, arithmetic and copies ran while one was open for 15% of the time, Pallas kernels for 19%

profile of v1, /device:TPU:32, one launch (start us, length us, event | category | flops | bytes accessed | tf_op | source)
XLA Modules:
  0.0 159.3 jit_solution(10409854900647501030)
XLA Ops:
  1.9 2.8 %fusion.8 = f32[1024,512]{1,0:T(8,128)S(1)} fusion(bf16[1024,512]{1,0:T(8,128)(2,1)S(1)} %copy-done, bf16[2,1024,1024]{2,1,0:T(8,128)(2,1)} %bitcast.53, s32[]{:T(128)S(6)} %select_n.15), kind=kOutput, calls=%fused_computation.16 | convolution fusion | flops 1073741824 | bytes 5242884 | tf_op jit(solution)/shard_map/dot_general | solution.py:170
  4.8 4.3 %collective-permute-done = f32[1024,512]{1,0:T(8,128)} collective-permute-done((f32[1024,512]{1,0:T(8,128)S(1)}, f32[1024,512]{1,0:T(8,128)}, u32[]{:S(2)}, u32[]{:S(2)}) %collective-permute-start) | collective-permute-done | bytes 2097184 | tf_op jit(solution)/shard_map/ppermute | solution.py:91
  9.1 4.1 %abs_reduce_fusion = (f32[]{:T(128)}, f32[1024,512]{1,0:T(8,128)S(1)}) fusion(f32[1024,512]{1,0:T(8,128)} %collective-permute-done, bf16[1024,512]{1,0:T(8,128)(2,1)S(1)} %copy-done, bf16[2,1024,1024]{2,1,0:T(8,128)(2,1)} %bitcast.54, s32[]{:T(128)S(6)} %select_n.14), kind=kOutput, calls=%fused_computation.30 | convolution fusion | flops 1075314688 | bytes 7340040 | tf_op jit(solution)/shard_map/dot_general | solution.py:170
  14.5 20.0 %all_to_all.30 = f16[4,264,512]{2,1,0:T(8,128)(2,1)S(1)} all-to-all(f16[4,264,512]{2,1,0:T(8,128)(2,1)S(1)} %concatenate.6), channel_id=1, replica_groups=mesh['tok_0'=4,'tok_1'=8,'feat_0'=4,'feat_1'=2] {'feat_0'}, dimensions={0} | all-to-all | bytes 2162688 | tf_op jit(solution)/shard_map/all_to_all | solution.py:82
  37.5 3.5 %all-to-all-start.1 = ((f16[4,264,512]{2,1,0:T(8,128)(2,1)}), f16[4,264,512]{2,1,0:T(8,128)(2,1)S(1)}, u32[]{:S(2)}, u32[]{:S(2)}) async-start(f16[4,264,512]{2,1,0:T(8,128)(2,1)} %broadcast_in_dim.8), calls=%async_computation.1 | async-start | bytes 2162688 | tf_op jit(solution)/shard_map/all_to_all | solution.py:82
  41.7 14.3 %all-to-all-done.1 = f16[4,264,512]{2,1,0:T(8,128)(2,1)S(1)} async-done(((f16[4,264,512]{2,1,0:T(8,128)(2,1)}), f16[4,264,512]{2,1,0:T(8,128)(2,1)S(1)}, u32[]{:S(2)}, u32[]{:S(2)}) %all-to-all-start.1) | async-done | bytes 1081376 | tf_op jit(solution)/shard_map/all_to_all | solution.py:82
  56.0 1.6 fusion.2
  57.6 1.7 %fusion = (bf16[1024,512]{1,0:T(8,128)(2,1)}, bf16[1024,512]{1,0:T(8,128)(2,1)}) fusion(f32[4,256,512]{2,1,0:T(8,128)S(1)} %get-tuple-element.18), kind=kLoop, calls=%fused_computation.8 | loop fusion | flops 2097152 | bytes 4194304 | tf_op jit(solution)/shard_map/convert_element_type | solution.py:109
  59.3 2.9 %share.1 = f32[128,512]{1,0:T(8,128)} custom-call(s32[2]{0:T(128)} %pad_add_fusion.place_ref, bf16[1024,512]{1,0:T(8,128)(2,1)} %get-tuple-element.12.high_ref.hm_ref, bf16[1024,512]{1,0:T(8,128)(2,1)} %get-tuple-element.11.low_ref.lm_ref), custom_call_target="tpu_custom_call" | custom-call | tf_op jit(solution)/shard_map/share/pallas_call | solution.py:178
  66.7 11.2 %all-to-all-start.2 = ((f32[32,2,512]{2,1,0:T(2,128)}), f32[32,2,512]{2,1,0:T(2,128)S(1)}, u32[]{:S(2)}, u32[]{:S(2)}) async-start(f32[32,2,512]{2,1,0:T(2,128)} %reshape.38), calls=%async_computation.2 | async-start | bytes 262144 | tf_op jit(solution)/shard_map/all_to_all | solution.py:82
  77.9 4.5 %fusion.12 = f32[1024,512]{1,0:T(8,128)} fusion(bf16[1024,512]{1,0:T(8,128)(2,1)} %bitcast.60, bf16[2,1024,1024]{2,1,0:T(8,128)(2,1)} %bitcast.55, s32[]{:T(128)S(6)} %select_n.14), kind=kOutput, calls=%fused_computation.20 | convolution fusion | flops 1073741824 | bytes 5242884 | tf_op jit(solution)/shard_map/dot_general | solution.py:195
  82.3 5.5 %all-to-all-done.2 = f32[32,2,512]{2,1,0:T(2,128)S(1)} async-done(((f32[32,2,512]{2,1,0:T(2,128)}), f32[32,2,512]{2,1,0:T(2,128)S(1)}, u32[]{:S(2)}, u32[]{:S(2)}) %all-to-all-start.2) | async-done | bytes 131104 | tf_op jit(solution)/shard_map/all_to_all | solution.py:82
  88.6 4.4 %all-to-all-start.3 = ((f32[32,2,512]{2,1,0:T(2,128)}), f32[32,2,512]{2,1,0:T(2,128)S(1)}, u32[]{:S(2)}, u32[]{:S(2)}) async-start(f32[32,2,512]{2,1,0:T(2,128)} %broadcast_in_dim.9), calls=%async_computation.3 | async-start | bytes 262144 | tf_op jit(solution)/shard_map/all_to_all | solution.py:82
  93.0 4.3 %fusion.10 = f32[1024,512]{1,0:T(8,128)} fusion(bf16[1024,512]{1,0:T(8,128)(2,1)S(1)} %bitcast.59, bf16[2,1024,1024]{2,1,0:T(8,128)(2,1)} %bitcast.56, s32[]{:T(128)S(6)} %select_n.14), kind=kOutput, calls=%fused_computation.18 | convolution fusion | flops 1073741824 | bytes 5242884 | tf_op jit(solution)/shard_map/dot_general | solution.py:195
  97.2 5.5 %all-to-all-done.3 = f32[32,2,512]{2,1,0:T(2,128)S(1)} async-done(((f32[32,2,512]{2,1,0:T(2,128)}), f32[32,2,512]{2,1,0:T(2,128)S(1)}, u32[]{:S(2)}, u32[]{:S(2)}) %all-to-all-start.3) | async-done | bytes 131104 | tf_op jit(solution)/shard_map/all_to_all | solution.py:82
  103.7 4.3 %all-to-all-start.4 = ((f32[4,64,512]{2,1,0:T(8,128)}), f32[4,64,512]{2,1,0:T(8,128)}, u32[]{:S(2)}, u32[]{:S(2)}) async-start(f32[4,64,512]{2,1,0:T(8,128)} %broadcast_in_dim.11), calls=%async_computation.4 | async-start | bytes 1048576 | tf_op jit(solution)/shard_map/all_to_all | solution.py:82
  108.9 1.9 %reduce-precision_convert_fusion = (bf16[4,256,512]{2,1,0:T(8,128)(2,1)S(1)}, bf16[4,256,512]{2,1,0:T(8,128)(2,1)S(1)}, f32[4,256,512]{2,1,0:T(8,128)S(1)}) fusion(f32[4]{0:T(128)S(1)} %fusion.38, f16[4,264,512]{2,1,0:T(8,128)(2,1)} %collective-permute-done.3), kind=kLoop, calls=%fused_computation.1 | loop fusion | flops 3145728 | bytes 5242896 | tf_op jit(solution)/shard_map/convert_element_type | solution.py:109
  113.6 2.3 %add_convert_fusion = bf16[1024,512]{1,0:T(8,128)(2,1)} fusion(f32[1024,512]{1,0:T(8,128)S(1)} %fusion.4, f32[1024,512]{1,0:T(8,128)S(1)} %copy-done.1, f32[1024,512]{1,0:T(8,128)S(1)} %copy-done.2, bf16[1024,512]{1,0:T(8,128)(2,1)S(1)} %bitcast.50, bf16[2,1024,1024]{2,1,0:T(8,128)(2,1)S(1)} %bitcast.58, s32[]{:T(128)S(6)} %select_n.15), kind=kOutput, calls=%fused_computation.25 | convolution fusion | flops 1075838976 | bytes 10485764 | tf_op jit(solution)/shard_map/dot_general | solution.py:195
  116.0 5.2 %all-to-all-start.5 = ((bf16[32,32,512]{2,1,0:T(8,128)(2,1)}), bf16[32,32,512]{2,1,0:T(8,128)(2,1)}, u32[]{:S(2)}, u32[]{:S(2)}) async-start(bf16[32,32,512]{2,1,0:T(8,128)(2,1)} %bitcast.49), calls=%async_computation.5 | async-start | bytes 2097152 | tf_op jit(solution)/shard_map/all_to_all | solution.py:82
  121.3 1.6 %fusion.1 = (bf16[1024,512]{1,0:T(8,128)(2,1)}, bf16[1024,512]{1,0:T(8,128)(2,1)}) fusion(f32[4,256,512]{2,1,0:T(8,128)S(1)} %get-tuple-element.15), kind=kLoop, calls=%fused_computation.9 | loop fusion | flops 2097152 | bytes 4194304 | tf_op jit(solution)/shard_map/convert_element_type | solution.py:109
  123.6 30.3 %basis.1 = (bf16[2048,512]{1,0:T(8,128)(2,1)}, f32[512,512]{1,0:T(8,128)}, f32[512,512]{1,0:T(8,128)}) custom-call(s32[2]{0:T(128)} %pad_add_fusion.place_ref, f32[4,64,512]{2,1,0:T(8,128)} %all-to-all-done.4.mine_ref, f32[4,64,512]{2,1,0:T(8,128)} %collective-permute-done.2.other_ref, bf16[1024,512]{1,0:T(8,128)(2,1)} %get-tuple-element.12.high_ref.hm_ref, ...), custom_call_target="tpu_custom_call" | custom-call | tf_op jit(solution)/shard_map/basis/pallas_call | solution.py:205
  153.9 2.4 %broadcast_multiply_fusion = f32[512,512]{1,0:T(8,128)} fusion(f32[512,512]{1,0:T(8,128)} %get-tuple-element.7), kind=kLoop, calls=%fused_computation.38 | loop fusion | flops 262144 | bytes 2097152 | tf_op jit(solution)/shard_map/div | solution.py:218
  156.3 1.4 convert_reduce_fusion
  157.6 1.7 %fusion.45 = f32[32,512]{1,0:T(8,128)} fusion(f32[32,512]{1,0:T(8,128)S(1)} %convert_reduce_fusion, f32[512,512]{1,0:T(8,128)S(1)} %copy-done.3), kind=kOutput, calls=%fused_computation.65 | convolution fusion | flops 100663296 | bytes 1179648 | tf_op jit(solution)/shard_map/dot_general | solution.py:219
  (38 shorter events, 15.5 us)
Async XLA Ops:
  0.6 1.2 copy-start
  4.7 4.4 %collective-permute-start = (f32[1024,512]{1,0:T(8,128)S(1)}, f32[1024,512]{1,0:T(8,128)}, u32[]{:S(2)}, u32[]{:S(2)}) collective-permute-start(f32[1024,512]{1,0:T(8,128)S(1)} %fusion.8), channel_id=1, source_target_pairs={{0,1},{1,0},{2,3},{3,2},{4,5},{5,4},{6,7},{7,6},{8,9},{9,8},{10,11... | collective-permute-start | bytes 6291464 | tf_op jit(solution)/shard_map/ppermute | solution.py:91
  37.5 18.4 %all-to-all-start.1 = ((f16[4,264,512]{2,1,0:T(8,128)(2,1)}), f16[4,264,512]{2,1,0:T(8,128)(2,1)S(1)}, u32[]{:S(2)}, u32[]{:S(2)}) async-start(f16[4,264,512]{2,1,0:T(8,128)(2,1)} %broadcast_in_dim.8), calls=%async_computation.1 | async-start | bytes 2162688 | tf_op jit(solution)/shard_map/all_to_all | solution.py:82
  62.1 45.9 %collective-permute-start.3 = (f16[4,264,512]{2,1,0:T(8,128)(2,1)S(1)}, f16[4,264,512]{2,1,0:T(8,128)(2,1)}, u32[]{:S(2)}, u32[]{:S(2)}) collective-permute-start(f16[4,264,512]{2,1,0:T(8,128)(2,1)S(1)} %all-to-all-done.1), channel_id=1, source_target_pairs={{0,1},{1,0},{2,3},{3,2},{4,5},{5,4},{6,7},{7,6},{8,9},{9,8},{10,11... | collective-permute-start | bytes 3244040 | tf_op jit(solution)/shard_map/ppermute | solution.py:91
  63.1 2.0 %collective-permute-start.1 = (f32[64,512]{1,0:T(8,128)S(1)}, f32[64,512]{1,0:T(8,128)S(1)}, u32[]{:S(2)}, u32[]{:S(2)}) collective-permute-start(f32[64,512]{1,0:T(8,128)S(1)} %dynamic-slice_bitcast_fusion), channel_id=1, source_target_pairs={{0,1},{1,0},{2,3},{3,2},{4,5},{5,4},{6,7},{7,6},{8,9},{9,8},{10,11... | collective-permute-start | bytes 393224 | tf_op jit(solution)/shard_map/ppermute | solution.py:91
  66.7 21.2 %all-to-all-start.2 = ((f32[32,2,512]{2,1,0:T(2,128)}), f32[32,2,512]{2,1,0:T(2,128)S(1)}, u32[]{:S(2)}, u32[]{:S(2)}) async-start(f32[32,2,512]{2,1,0:T(2,128)} %reshape.38), calls=%async_computation.2 | async-start | bytes 262144 | tf_op jit(solution)/shard_map/all_to_all | solution.py:82
  88.6 14.1 %all-to-all-start.3 = ((f32[32,2,512]{2,1,0:T(2,128)}), f32[32,2,512]{2,1,0:T(2,128)S(1)}, u32[]{:S(2)}, u32[]{:S(2)}) async-start(f32[32,2,512]{2,1,0:T(2,128)} %broadcast_in_dim.9), calls=%async_computation.3 | async-start | bytes 262144 | tf_op jit(solution)/shard_map/all_to_all | solution.py:82
  103.7 12.3 %all-to-all-start.4 = ((f32[4,64,512]{2,1,0:T(8,128)}), f32[4,64,512]{2,1,0:T(8,128)}, u32[]{:S(2)}, u32[]{:S(2)}) async-start(f32[4,64,512]{2,1,0:T(8,128)} %broadcast_in_dim.11), calls=%async_computation.4 | async-start | bytes 1048576 | tf_op jit(solution)/shard_map/all_to_all | solution.py:82
  108.9 2.5 %copy-start.4 = (bf16[2048,1024]{1,0:T(8,128)(2,1)S(1)}, bf16[2048,1024]{1,0:T(8,128)(2,1)}, u32[]{:S(2)}) copy-start(bf16[2048,1024]{1,0:T(8,128)(2,1)} %param.2) | copy-start | bytes 12582916
  111.4 1.6 copy-start.1
  111.4 2.2 %copy-start.2 = (f32[1024,512]{1,0:T(8,128)S(1)}, f32[1024,512]{1,0:T(8,128)}, u32[]{:S(2)}) copy-start(f32[1024,512]{1,0:T(8,128)} %fusion.10) | copy-start | bytes 6291460
  116.0 40.2 %all-to-all-start.5 = ((bf16[32,32,512]{2,1,0:T(8,128)(2,1)}), bf16[32,32,512]{2,1,0:T(8,128)(2,1)}, u32[]{:S(2)}, u32[]{:S(2)}) async-start(bf16[32,32,512]{2,1,0:T(8,128)(2,1)} %bitcast.49), calls=%async_computation.5 | async-start | bytes 2097152 | tf_op jit(solution)/shard_map/all_to_all | solution.py:82
  121.2 2.3 %collective-permute-start.2 = (f32[4,64,512]{2,1,0:T(8,128)}, f32[4,64,512]{2,1,0:T(8,128)}, u32[]{:S(2)}, u32[]{:S(2)}) collective-permute-start(f32[4,64,512]{2,1,0:T(8,128)} %all-to-all-done.4.mine_ref), channel_id=1, source_target_pairs={{0,1},{1,0},{2,3},{3,2},{4,5},{5,4},{6,7},{7,6},{8,9},{9,8},{10,11... | collective-permute-start | bytes 1572872 | tf_op jit(solution)/shard_map/ppermute | solution.py:91
  153.9 3.8 %copy-start.3 = (f32[512,512]{1,0:T(8,128)S(1)}, f32[512,512]{1,0:T(8,128)}, u32[]{:S(2)}) copy-start(f32[512,512]{1,0:T(8,128)} %get-tuple-element.8) | copy-start | bytes 3145732

commit v2 on v1

v2 whole, which is shorter than its diff:
```python
import functools
import math

import jax
import jax.numpy as jnp
from jax import lax
from jax.experimental import pallas as pl
from jax.experimental.pallas import tpu as pltpu
from jax.sharding import Mesh
from jax.sharding import PartitionSpec as P

HIGH = lax.Precision.HIGHEST
NB, PB = 128, 8


def row_of(tile, k):
    return jnp.broadcast_to(tile[k : k + 1, :], (PB, NB))


def diag_factor(block):
    sub = lax.broadcasted_iota(jnp.int32, (PB, NB), 0)
    lane = lax.broadcasted_iota(jnp.int32, (PB, NB), 1)
    n = NB // PB
    xs = [block[PB * p : PB * (p + 1), :] for p in range(n)]
    vs = [jnp.where(lane == sub + PB * p, 1.0, 0.0).astype(jnp.float32) for p in range(n)]
    for p in range(0, n, 2):
        first = PB * p
        x, v = xs[p : p + 2], vs[p : p + 2]
        cols = [
            [jnp.broadcast_to(x[h][:, first + k : first + k + 1], (PB, NB)) for h in range(2)]
            for k in range(2 * PB)
        ]
        scale = [jnp.ones((PB, NB), jnp.float32)] * 2
        for k in range(2 * PB):
            h, i = divmod(k, PB)
            pivot = row_of(cols[k][h], i)
            below = {h: jnp.where(sub > i, cols[k][h], 0.0)}
            if h == 0:
                below[1] = cols[k][1]
            r = lax.rsqrt(pivot)
            square = r * r
            if k + 1 < 2 * PB:
                head = row_of(cols[k + 1][h], i)
                for g in below:
                    cols[k + 1][g] = cols[k + 1][g] - (below[g] * head) * square
            coef = {g: below[g] * square for g in below}
            scale[h] = jnp.where(sub == i, r, scale[h])
            for j in range(k + 2, 2 * PB):
                head = row_of(cols[j][h], i)
                for g in below:
                    cols[j][g] = cols[j][g] - coef[g] * head
            for m in (x, v):
                head = row_of(m[h], i)
                for g in below:
                    m[g] = m[g] - coef[g] * head
        for h in range(2):
            x[h], v[h] = x[h] * scale[h], v[h] * scale[h]
        xs[p : p + 2], vs[p : p + 2] = x, v
        for q in range(p + 2, n):
            pick = lane == sub + PB * q
            for k in range(2 * PB):
                h, i = divmod(k, PB)
                row = row_of(x[h], i)
                c = jnp.sum(jnp.where(pick, row, 0.0), axis=1, keepdims=True)
                xs[q] = xs[q] - c * row
                vs[q] = vs[q] - c * row_of(v[h], i)
    rows = [jnp.where(lane >= sub + PB * p, xs[p], 0.0) for p in range(n)]
    return jnp.concatenate(rows, 0), jnp.concatenate(vs, 0)


def tn(a, b):
    return lax.dot_general(
        a, b, (((0,), (0,)), ((), ())), precision=HIGH, preferred_element_type=jnp.float32
    )


def nn(a, b):
    return jnp.dot(a, b, precision=HIGH, preferred_element_type=jnp.float32)


def factor_in_place(s_ref, r_ref, w_ref):
    n = s_ref.shape[0] // NB

    def at(i):
        return slice(NB * i, NB * (i + 1))

    r_ref[...] = jnp.zeros_like(r_ref)
    w_ref[...] = jnp.zeros_like(w_ref)
    def factor_block(b, _):
        here = pl.ds(pl.multiple_of(b * NB, NB), NB)
        upper, inv = diag_factor(s_ref[here, here])
        r_ref[here, here] = upper
        w_ref[here, here] = inv
        for i in range(n):
            pl.when(b == i)(functools.partial(after_block, i))
        return 0

    def after_block(b):
        inv = w_ref[at(b), at(b)]
        if b < n - 1:
            rest = slice(NB * (b + 1), NB * n)
            r_ref[at(b), rest] = nn(inv, s_ref[at(b), rest])
            for j in range(b + 1, n):
                tail = slice(NB * j, NB * n)
                s_ref[at(j), tail] = s_ref[at(j), tail] - tn(r_ref[at(b), at(j)], r_ref[at(b), tail])
        if b:
            left = tn(r_ref[0 : NB * b, at(b)], w_ref[0 : NB * b, 0 : NB * b])
            w_ref[at(b), 0 : NB * b] = -nn(inv, left)

    lax.fori_loop(0, n, factor_block, 0)

X, Z, Y, C = "tok_0", "tok_1", "feat_0", "feat_1"
TOK = (X, Z)
LEVEL = 14.0
TAIL = 8
F32, BF16, F16 = jnp.float32, jnp.bfloat16, jnp.float16
VMEM = pl.BlockSpec(memory_space=pltpu.VMEM)
SMEM = pl.BlockSpec(memory_space=pltpu.SMEM)


def struct(shape, dtype):
    return jax.ShapeDtypeStruct(shape, dtype)


def exchange(blocks, axis):
    return lax.all_to_all(blocks, axis, 0, 0, tiled=True)


def shifted(array, axis, shift):
    peers = lax.axis_size(axis)
    return lax.ppermute(array, axis, [(i, (i + shift) % peers) for i in range(peers)])


def flipped(array, axis, bit):
    return lax.ppermute(array, axis, [(i, i ^ bit) for i in range(lax.axis_size(axis))])


def from_partner(array):
    return flipped(array, C, 1)


def block_of(blocks, i):
    return lax.dynamic_index_in_dim(blocks, i, 0, keepdims=False)


def packed(values, power):
    tail = jnp.full((TAIL, values.shape[1]), power.astype(F16))
    return jnp.concatenate([(values * jnp.exp2(LEVEL - power)).astype(F16), tail])


def unpacked(block):
    rows = block.shape[0] - TAIL
    power = block[rows, 0].astype(F32)
    return block[:rows].astype(F32) * jnp.exp2(power - LEVEL), power


def split(values):
    high = lax.reduce_precision(values, 8, 7)
    return high.astype(BF16), (values - high).astype(BF16)


def dot_tn(a, b):
    return lax.dot_general(a, b, (((0,), (0,)), ((), ())), preferred_element_type=F32)


def dot_nn(a, b):
    return jnp.dot(a, b, preferred_element_type=F32)


def part(i, size):
    return pl.ds(pl.multiple_of(i * size, size), size)


def share_kernel(place_ref, *refs):
    highs, lows = refs[0:4], refs[4:8]
    high_ref, low_ref, kept_ref, given_ref, strip_ref = refs[8:]
    core, row = place_ref[0], place_ref[1]
    block = highs[0].shape[0]
    for s in range(4):
        at = part(lax.rem(row + 4 - s, 4), block)
        high_ref[at, :] = highs[s][...]
        low_ref[at, :] = lows[s][...]
    strip, half = strip_ref.shape[0], kept_ref.shape[0]
    lanes = part(row, strip)
    high, low = high_ref[...], low_ref[...]
    strip_ref[...] = dot_tn(high_ref[:, lanes], high) + (
        dot_tn(high_ref[:, lanes], low) + dot_tn(low_ref[:, lanes], high)
    )
    kept_ref[...] = strip_ref[part(core, half), :]
    given_ref[...] = strip_ref[part(1 - core, half), :]


def basis_kernel(scale, place_ref, *refs):
    mine, other = refs[0:4], refs[4:8]
    hm_ref, lm_ref, ho_ref, lo_ref, q_ref, out_ref, uh_ref, ul_ref, s_ref, r_ref, w_ref = refs[8:]
    core, row = place_ref[0], place_ref[1]
    half = mine[0].shape[0]
    columns = s_ref.shape[0]
    for s in range(4):
        strip = 2 * lax.rem(row + 4 - s, 4)
        s_ref[part(strip + core, half), :] = mine[s][...]
        s_ref[part(strip + 1 - core, half), :] = other[s][...]
    factor_in_place(s_ref, r_ref, w_ref)
    out_ref[...] = r_ref[...] * scale
    for j in range(0, columns, NB):
        u = w_ref[j : j + NB, :].T
        high = u.astype(BF16)
        uh_ref[:, j : j + NB] = high
        ul_ref[:, j : j + NB] = (u - high.astype(F32)).astype(BF16)
    rows = hm_ref.shape[0]
    step = 256
    for place, h_ref, l_ref in ((core, hm_ref, lm_ref), (1 - core, ho_ref, lo_ref)):

        def some_rows(i, _, place=place, h_ref=h_ref, l_ref=l_ref):
            at, out = part(i, step), part(place * (rows // step) + i, step)
            for j in range(0, columns, 256):
                k = j + 256
                h, l = h_ref[at, :k], l_ref[at, :k]
                uh, ul = uh_ref[:k, j:k], ul_ref[:k, j:k]
                q_ref[out, j:k] = (dot_nn(h, uh) + (dot_nn(h, ul) + dot_nn(l, uh))).astype(BF16)
            return 0

        lax.fori_loop(0, rows // step, some_rows, 0)


def image_kernel(in_ref, uh_ref, ul_ref, out_ref):
    total = in_ref[0].astype(F32)
    for i in range(1, in_ref.shape[0]):
        total = total + in_ref[i].astype(F32)
    high = total.astype(BF16)
    low = (total - high.astype(F32)).astype(BF16)
    uh = uh_ref[...]
    out_ref[...] = dot_nn(high, uh) + (dot_nn(high, ul_ref[...]) + dot_nn(low, uh))


def body(slab, sketch):
    core, row = lax.axis_index(C), lax.axis_index(Y)
    place = jnp.stack([core, row]).astype(jnp.int32)
    tokens, columns = slab.shape[0], sketch.shape[1]
    half, block, strip = tokens // 2, tokens // 8, columns // 4
    halves = slab.reshape(2, half, slab.shape[1])

    def partial(which):
        return jnp.dot(block_of(halves, which), sketch, preferred_element_type=F32)

    theirs = from_partner(partial(1 - core))
    mine = lax.optimization_barrier(partial(core))
    pair_sum = (mine + theirs).reshape(4, block, columns)
    power = jnp.clip(jnp.floor(jnp.log2(jnp.max(jnp.abs(pair_sum)))), -100.0, 40.0)
    own, top = block_of(pair_sum, row), power
    for s in range(1, 4):
        sent = packed(block_of(pair_sum, (row + s) % 4), power)
        values, its_power = unpacked(shifted(sent, Y, s))
        own, top = own + values, jnp.maximum(top, its_power)
    message = packed(own, top + 2.0)
    pieces = [split(unpacked(message)[0])]
    pieces += [split(unpacked(shifted(message, Y, s))[0]) for s in range(1, 4)]

    pair = struct((half, columns), BF16)
    slice_of = struct((strip // 2, columns), F32)
    high_mine, low_mine, kept, given = pl.pallas_call(
        share_kernel,
        out_shape=(pair, pair, slice_of, slice_of),
        in_specs=[SMEM] + [VMEM] * 8,
        out_specs=(VMEM,) * 4,
        scratch_shapes=[pltpu.VMEM((strip, columns), F32)],
        compiler_params=pltpu.CompilerParams(vmem_limit_bytes=16 << 20),
        name="share",
    )(place, *[p[0] for p in pieces], *[p[1] for p in pieces])
    strip_sum = kept + from_partner(given)
    high_other, low_other = from_partner(high_mine), from_partner(low_mine)

    summed = exchange(strip_sum.reshape(8, -1, columns), Z).sum(axis=0)
    summed = (summed + flipped(summed, X, 1)) + (flipped(summed, X, 2) + flipped(summed, X, 3))
    done = exchange(jnp.broadcast_to(summed[None], (8, *summed.shape)), Z).reshape(-1, columns)

    def onto(which, values):
        return dot_tn(block_of(halves, which), values)

    images = onto(core, high_mine) + onto(core, low_mine)
    images = images + (onto(1 - core, high_other) + onto(1 - core, low_other))
    image = exchange(images.astype(BF16).reshape(32, -1, columns), TOK)

    strips = [done] + [shifted(done, Y, s) for s in range(1, 4)]
    square = struct((columns, columns), BF16)
    token_count = tokens * lax.axis_size(TOK)
    q_basis, r_scaled, upper_high, upper_low = pl.pallas_call(
        functools.partial(basis_kernel, 1.0 / math.sqrt(token_count)),
        out_shape=(
            struct((tokens, columns), BF16), struct((columns, columns), F32), square, square
        ),
        in_specs=[SMEM] + [VMEM] * 12,
        out_specs=(VMEM,) * 4,
        scratch_shapes=[pltpu.VMEM((columns, columns), F32)] * 3,
        compiler_params=pltpu.CompilerParams(vmem_limit_bytes=24 << 20),
        name="basis",
    )(place, *strips, *[from_partner(s) for s in strips], high_mine, low_mine, high_other, low_other)
    projected = pl.pallas_call(
        image_kernel,
        out_shape=struct((image.shape[1], columns), F32),
        in_specs=[VMEM] * 3,
        out_specs=VMEM,
        compiler_params=pltpu.CompilerParams(vmem_limit_bytes=8 << 20),
        name="image",
    )(image, upper_high, upper_low)
    return (q_basis, r_scaled, projected)


def solution(mesh):
    split_mesh = Mesh(mesh.devices.reshape(4, 8, 4, 2), (X, Z, Y, C))
    in_specs = (P(TOK, (Y, C)), P((Y, C), None))
    out_specs = (P(TOK, None), P(), P((Y, C, X, Z), None))
    return jax.shard_map(body, mesh=split_mesh, in_specs=in_specs, out_specs=out_specs, check_vma=False)
```

time: 162 us -> 151 us (0.932)
  blocking collectives: 20 us -> 0 us
  starting transfers between devices: 29.3 us -> 41.8 us
  other arithmetic: 14.5 us -> 5.98 us
  local copies, waits for them, and re-layouts: 7.33 us -> 13.5 us
  Pallas kernels: 33.2 us -> 27.2 us
  between operations: 2.28 us -> 5.9 us
  matrix products: 20.9 us -> 22.9 us
    ppermute x4 -> x20, waiting for transfers between devices: 6.26 us -> 28.2 us  [the longest x9 26 us: shifted(): lax.ppermute(array, axis, [(i, (i + shift) % peers) for i in range(peers)])]
    all_to_all x5 -> x3, waiting for transfers between devices: 25.5 us -> 3.84 us  [exchange(): return lax.all_to_all(blocks, axis, 0, 0, tiled=True)]
    all_to_all x1 -> x0, blocking collectives: 20 us -> none  [exchange(): return lax.all_to_all(blocks, axis, 0, 0, tiled=True)]
    ppermute x4 -> x20, starting transfers between devices: 0.78 us -> 19.3 us  [the longest x9 13.7 us: shifted(): lax.ppermute(array, axis, [(i, (i + shift) % peers) for i in range(peers)])]
    all_to_all x5 -> x3, starting transfers between devices: 28.5 us -> 22.5 us  [exchange(): return lax.all_to_all(blocks, axis, 0, 0, tiled=True)]
    pallas_call x2 -> x3, Pallas kernels: 33.2 us -> 27.2 us  [the longest x1 23.9 us: body(): pl.pallas_call(functools.partial(basis_kernel, 1.0 / math.sqrt(token_coun...]
    convert_element_type x4 -> x5, other arithmetic: 6.8 us -> 1.7 us  [split(): return (high.astype(BF16), (values - high).astype(BF16))]
    slice x0 -> x6, local copies, waits for them, and re-layouts: none -> 5.1 us  [unpacked(): power = block[rows, 0].astype(F32)]
  transfers between devices with their start and end apart: 9 -> 23, of which waited for: 7 -> 12; matrix products, arithmetic and copies ran while one was open for 15% -> 17% of each run, Pallas kernels for 19% -> 16%
where the time goes in v2:
time: 151 us; the launch traced here: 149 us
  starting transfers between devices  41.8 us (28%)
  waiting for transfers between devices  32.1 us (21%)
  Pallas kernels  27.2 us (18%)
  matrix products  22.9 us (15%)
  local copies, waits for them, and re-layouts  13.5 us (9%)
  other arithmetic  5.98 us (4%)
  between operations  5.9 us (4%)
    ppermute x9, waiting for transfers between devices, shifted(): lax.ppermute(array, axis, [(i, (i + shift) % peers) for i in range(peers)])  26 us
    pallas_call x1, Pallas kernels, body(): pl.pallas_call(functools.partial(basis_kernel, 1.0 / math.sqrt(token_coun...  23.9 us
    all_to_all x3, starting transfers between devices, exchange(): return lax.all_to_all(blocks, axis, 0, 0, tiled=True)  22.5 us
    dot_general x4, matrix products, dot_tn(): lax.dot_general(a, b, (((0,), (0,)), ((), ())), preferred_element_type=F32)  15.9 us
    ppermute x9, starting transfers between devices, shifted(): lax.ppermute(array, axis, [(i, (i + shift) % peers) for i in range(peers)])  13.7 us
    dot_general x2, matrix products, partial(): return jnp.dot(block_of(halves, which), sketch, preferred_element_type=F32)  6.99 us
    unnamed x18, local copies, waits for them, and re-layouts  6.11 us
    ppermute x11, starting transfers between devices, flipped(): lax.ppermute(array, axis, [(i, i ^ bit) for i in range(lax.axis_size(axis...  5.58 us
  transfers between devices with their start and end apart: 23, of which 12 were waited for; matrix products, arithmetic and copies ran while one was open for 17% of the time, Pallas kernels for 16%

profile of v2, /device:TPU:32, one launch (start us, length us, event | category | flops | bytes accessed | tf_op | source)
XLA Modules:
  0.0 149.2 jit_solution(1196845120083726541)
XLA Ops:
  1.9 2.8 %fusion.4 = f32[1024,512]{1,0:T(8,128)S(1)} fusion(bf16[1024,512]{1,0:T(8,128)(2,1)S(1)} %copy-done, bf16[2,1024,1024]{2,1,0:T(8,128)(2,1)} %bitcast.64, s32[]{:T(128)S(6)} %select_n.40), kind=kOutput, calls=%fused_computation.4 | convolution fusion | flops 1073741824 | bytes 5242884 | tf_op jit(solution)/shard_map/dot_general | solution.py:244
  4.8 4.2 %fusion.10 = f32[1024,512]{1,0:T(8,128)} fusion(bf16[1024,512]{1,0:T(8,128)(2,1)S(1)} %copy-done, bf16[2,1024,1024]{2,1,0:T(8,128)(2,1)} %bitcast.65, s32[]{:T(128)S(6)} %select_n.39), kind=kOutput, calls=%fused_computation.10 | convolution fusion | flops 1073741824 | bytes 5242884 | tf_op jit(solution)/shard_map/dot_general | solution.py:244
  9.1 3.3 %abs_reduce_fusion = (f32[]{:T(128)}, f32[1024,512]{1,0:T(8,128)S(1)}) fusion(f32[1024,512]{1,0:T(8,128)} %fusion.10, f32[1024,512]{1,0:T(8,128)} %collective-permute-done), kind=kLoop, calls=%fused_computation.13 | loop fusion | flops 1572863 | bytes 6291460 | tf_op jit(solution)/shard_map/reduce_max | solution.py:249
  14.1 3.0 %collective-permute-start.3 = (f16[264,512]{1,0:T(8,128)(2,1)}, f16[264,512]{1,0:T(8,128)(2,1)}, u32[]{:S(2)}, u32[]{:S(2)}) collective-permute-start(f16[264,512]{1,0:T(8,128)(2,1)} %concatenate.14), channel_id=1, source_target_pairs={{0,6},{2,0},{4,2},{6,4},{1,7},{3,1},{5,3},{7,5},{8,14},{10,8},{12,... | collective-permute-start | bytes 811016 | tf_op jit(solution)/shard_map/ppermute | solution.py:131
  19.6 9.9 %collective-permute-done.3 = f16[264,512]{1,0:T(8,128)(2,1)} collective-permute-done((f16[264,512]{1,0:T(8,128)(2,1)}, f16[264,512]{1,0:T(8,128)(2,1)}, u32[]{:S(2)}, u32[]{:S(2)}) %collective-permute-start.3) | collective-permute-done | bytes 270368 | tf_op jit(solution)/shard_map/ppermute | solution.py:131
  35.3 1.4 fusion.20
  36.7 3.8 %collective-permute-start.6 = (f16[264,512]{1,0:T(8,128)(2,1)S(1)}, f16[264,512]{1,0:T(8,128)(2,1)S(1)}, u32[]{:S(2)}, u32[]{:S(2)}) collective-permute-start(f16[264,512]{1,0:T(8,128)(2,1)S(1)} %concatenate.15), channel_id=1, source_target_pairs={{0,6},{2,0},{4,2},{6,4},{1,7},{3,1},{5,3},{7,5},{8,14},{10,8},{12,... | collective-permute-start | bytes 811016 | tf_op jit(solution)/shard_map/ppermute | solution.py:131
  41.6 10.1 %collective-permute-done.6 = f16[264,512]{1,0:T(8,128)(2,1)S(1)} collective-permute-done((f16[264,512]{1,0:T(8,128)(2,1)S(1)}, f16[264,512]{1,0:T(8,128)(2,1)S(1)}, u32[]{:S(2)}, u32[]{:S(2)}) %collective-permute-start.6) | collective-permute-done | bytes 270368 | tf_op jit(solution)/shard_map/ppermute | solution.py:131
  56.6 2.2 %share.1 = (bf16[1024,512]{1,0:T(8,128)(2,1)S(1)}, bf16[1024,512]{1,0:T(8,128)(2,1)}, f32[64,512]{1,0:T(8,128)S(1)}, f32[64,512]{1,0:T(8,128)S(1)}) custom-call(s32[2]{0:T(128)S(1)} %pad_add_fusion.place_ref, bf16[256,512]{1,0:T(8,128)(2,1)S(1)} %reduce-precision_convert_fusion.3.refs_0_, bf16[256,512]{1,0:T(8,128)(2,1)S(1)} %get-tuple-element.31.refs_1_, ...), custom_call_target="tpu_custom_call" | custom-call | tf_op jit(solution)/shard_map/share/pallas_call | solution.py:261
  60.8 8.6 %all-to-all-start = ((f32[8,8,512]{2,1,0:T(8,128)}), f32[8,8,512]{2,1,0:T(8,128)S(1)}, u32[]{:S(2)}, u32[]{:S(2)}) async-start(f32[8,8,512]{2,1,0:T(8,128)} %add_bitcast_fusion), calls=%async_computation | async-start | bytes 262144 | tf_op jit(solution)/shard_map/all_to_all | solution.py:126
  69.4 4.5 %fusion.6 = f32[1024,512]{1,0:T(8,128)} fusion(bf16[1024,512]{1,0:T(8,128)(2,1)} %get-tuple-element.14.refs_9_, bf16[2,1024,1024]{2,1,0:T(8,128)(2,1)} %bitcast.66, s32[]{:T(128)S(6)} %select_n.39), kind=kOutput, calls=%fused_computation.6 | convolution fusion | flops 1073741824 | bytes 5242884 | tf_op jit(solution)/shard_map/dot_general | solution.py:163
  73.9 3.4 %all-to-all-done = f32[8,8,512]{2,1,0:T(8,128)S(1)} async-done(((f32[8,8,512]{2,1,0:T(8,128)}), f32[8,8,512]{2,1,0:T(8,128)S(1)}, u32[]{:S(2)}, u32[]{:S(2)}) %all-to-all-start) | async-done | bytes 131104 | tf_op jit(solution)/shard_map/all_to_all | solution.py:126
  77.3 3.0 %collective-permute-start.10 = (f32[8,512]{1,0:T(8,128)S(1)}, f32[8,512]{1,0:T(8,128)S(1)}, u32[]{:S(2)}, u32[]{:S(2)}) collective-permute-start(f32[8,512]{1,0:T(8,128)S(1)} %reduce_sum.9), channel_id=1, source_target_pairs={{0,192},{64,128},{128,64},{192,0},{1,193},{65,129},{129,65},{193,1... | collective-permute-start | bytes 49160 | tf_op jit(solution)/shard_map/ppermute | solution.py:135
  80.6 1.7 %collective-permute-start.9 = (f32[8,512]{1,0:T(8,128)S(1)}, f32[8,512]{1,0:T(8,128)S(1)}, u32[]{:S(2)}, u32[]{:S(2)}) collective-permute-start(f32[8,512]{1,0:T(8,128)S(1)} %reduce_sum.9), channel_id=1, source_target_pairs={{0,128},{64,192},{128,0},{192,64},{1,129},{65,193},{129,1},{193,65... | collective-permute-start | bytes 49160 | tf_op jit(solution)/shard_map/ppermute | solution.py:135
  82.3 4.2 %fusion.8 = f32[1024,512]{1,0:T(8,128)} fusion(bf16[1024,512]{1,0:T(8,128)(2,1)S(1)} %get-tuple-element.13.refs_8_, bf16[2,1024,1024]{2,1,0:T(8,128)(2,1)} %bitcast.67, s32[]{:T(128)S(6)} %select_n.39), kind=kOutput, calls=%fused_computation.8 | convolution fusion | flops 1073741824 | bytes 5242884 | tf_op jit(solution)/shard_map/dot_general | solution.py:163
  87.2 4.7 %all-to-all-start.1 = ((f32[8,8,512]{2,1,0:T(8,128)}), f32[8,8,512]{2,1,0:T(8,128)S(1)}, u32[]{:S(2)}, u32[]{:S(2)}) async-start(f32[8,8,512]{2,1,0:T(8,128)} %broadcast_in_dim.2), calls=%async_computation.1 | async-start | bytes 262144 | tf_op jit(solution)/shard_map/all_to_all | solution.py:126
  91.9 3.3 %fusion = f32[1024,512]{1,0:T(8,128)S(1)} fusion(bf16[1024,512]{1,0:T(8,128)(2,1)} %collective-permute-done.19.refs_11_, bf16[2,1024,1024]{2,1,0:T(8,128)(2,1)} %bitcast.68, s32[]{:T(128)S(6)} %select_n.40), kind=kOutput, calls=%fused_computation | convolution fusion | flops 1073741824 | bytes 5242884 | tf_op jit(solution)/shard_map/dot_general | solution.py:163
  95.3 3.9 %add_convert_fusion = bf16[1024,512]{1,0:T(8,128)(2,1)} fusion(f32[1024,512]{1,0:T(8,128)S(1)} %fusion, f32[1024,512]{1,0:T(8,128)S(1)} %copy-done.8, f32[1024,512]{1,0:T(8,128)S(1)} %copy-done.7, bf16[1024,512]{1,0:T(8,128)(2,1)S(1)} %collective-permute-done.18.refs_10_, bf16[2,1024,1024]{2,1,0:T(8,128)(2,1)} %bitcast.69, s32[]{:T(128)S(6)} %select_n.40), kind=kOutput, calls=%fused_computation.12 | convolution fusion | flops 1075838976 | bytes 10485764 | tf_op jit(solution)/shard_map/dot_general | solution.py:163
  99.6 9.2 %all-to-all-start.2 = ((bf16[32,32,512]{2,1,0:T(8,128)(2,1)}), bf16[32,32,512]{2,1,0:T(8,128)(2,1)S(1)}, u32[]{:S(2)}, u32[]{:S(2)}) async-start(bf16[32,32,512]{2,1,0:T(8,128)(2,1)} %bitcast.63), calls=%async_computation.2 | async-start | bytes 2097152 | tf_op jit(solution)/shard_map/all_to_all | solution.py:126
  108.8 4.2 %collective-permute-start.12 = (f32[64,512]{1,0:T(8,128)S(1)}, f32[64,512]{1,0:T(8,128)S(1)}, u32[]{:S(2)}, u32[]{:S(2)}) collective-permute-start(f32[64,512]{1,0:T(8,128)S(1)} %bitcast.57), channel_id=1, source_target_pairs={{0,4},{2,6},{4,0},{6,2},{1,5},{3,7},{5,1},{7,3},{8,12},{10,14},{12... | collective-permute-start | bytes 393224 | tf_op jit(solution)/shard_map/ppermute | solution.py:131
  113.0 2.0 %collective-permute-done.11.refs_1_ = f32[64,512]{1,0:T(8,128)S(1)} collective-permute-done((f32[64,512]{1,0:T(8,128)S(1)}, f32[64,512]{1,0:T(8,128)S(1)}, u32[]{:S(2)}, u32[]{:S(2)}) %collective-permute-start.11) | collective-permute-done | bytes 131104 | tf_op jit(solution)/shard_map/ppermute | solution.py:131
  115.0 2.4 %collective-permute-done.12.refs_2_ = f32[64,512]{1,0:T(8,128)S(1)} collective-permute-done((f32[64,512]{1,0:T(8,128)S(1)}, f32[64,512]{1,0:T(8,128)S(1)}, u32[]{:S(2)}, u32[]{:S(2)}) %collective-permute-start.12) | collective-permute-done | bytes 131104 | tf_op jit(solution)/shard_map/ppermute | solution.py:131
  119.3 1.2 copy-done.2
  120.6 23.9 %basis.1 = (bf16[2048,512]{1,0:T(8,128)(2,1)}, f32[512,512]{1,0:T(8,128)}, bf16[512,512]{1,0:T(8,128)(2,1)S(1)}, bf16[512,512]{1,0:T(8,128)(2,1)S(1)}) custom-call(s32[2]{0:T(128)S(1)} %pad_add_fusion.place_ref, f32[64,512]{1,0:T(8,128)S(1)} %bitcast.60, f32[64,512]{1,0:T(8,128)S(1)} %collective-permute-done.11.refs_1_, ...), custom_call_target="tpu_custom_call" | custom-call | tf_op jit(solution)/shard_map/basis/pallas_call | solution.py:287
  (71 shorter events, 22.5 us)
Async XLA Ops:
  4.7 4.4 %collective-permute-start = (f32[1024,512]{1,0:T(8,128)S(1)}, f32[1024,512]{1,0:T(8,128)}, u32[]{:S(2)}, u32[]{:S(2)}) collective-permute-start(f32[1024,512]{1,0:T(8,128)S(1)} %fusion.4), channel_id=1, source_target_pairs={{0,1},{1,0},{2,3},{3,2},{4,5},{5,4},{6,7},{7,6},{8,9},{9,8},{10,11... | collective-permute-start | bytes 6291464 | tf_op jit(solution)/shard_map/ppermute | solution.py:135
  14.1 15.4 %collective-permute-start.3 = (f16[264,512]{1,0:T(8,128)(2,1)}, f16[264,512]{1,0:T(8,128)(2,1)}, u32[]{:S(2)}, u32[]{:S(2)}) collective-permute-start(f16[264,512]{1,0:T(8,128)(2,1)} %concatenate.14), channel_id=1, source_target_pairs={{0,6},{2,0},{4,2},{6,4},{1,7},{3,1},{5,3},{7,5},{8,14},{10,8},{12,... | collective-permute-start | bytes 811016 | tf_op jit(solution)/shard_map/ppermute | solution.py:131
  17.2 14.2 %collective-permute-start.2 = (f16[264,512]{1,0:T(8,128)(2,1)S(1)}, f16[264,512]{1,0:T(8,128)(2,1)}, u32[]{:S(2)}, u32[]{:S(2)}) collective-permute-start(f16[264,512]{1,0:T(8,128)(2,1)S(1)} %concatenate.13), channel_id=1, source_target_pairs={{0,4},{2,6},{4,0},{6,2},{1,5},{3,7},{5,1},{7,3},{8,12},{10,14},{12... | collective-permute-start | bytes 811016 | tf_op jit(solution)/shard_map/ppermute | solution.py:131
  18.6 14.6 %collective-permute-start.1 = (f16[264,512]{1,0:T(8,128)(2,1)}, f16[264,512]{1,0:T(8,128)(2,1)}, u32[]{:S(2)}, u32[]{:S(2)}) collective-permute-start(f16[264,512]{1,0:T(8,128)(2,1)} %concatenate.12), channel_id=1, source_target_pairs={{0,2},{2,4},{4,6},{6,0},{1,3},{3,5},{5,7},{7,1},{8,10},{10,12},{12... | collective-permute-start | bytes 811016 | tf_op jit(solution)/shard_map/ppermute | solution.py:131
  36.7 15.0 %collective-permute-start.6 = (f16[264,512]{1,0:T(8,128)(2,1)S(1)}, f16[264,512]{1,0:T(8,128)(2,1)S(1)}, u32[]{:S(2)}, u32[]{:S(2)}) collective-permute-start(f16[264,512]{1,0:T(8,128)(2,1)S(1)} %concatenate.15), channel_id=1, source_target_pairs={{0,6},{2,0},{4,2},{6,4},{1,7},{3,1},{5,3},{7,5},{8,14},{10,8},{12,... | collective-permute-start | bytes 811016 | tf_op jit(solution)/shard_map/ppermute | solution.py:131
  40.5 12.4 %collective-permute-start.5 = (f16[264,512]{1,0:T(8,128)(2,1)S(1)}, f16[264,512]{1,0:T(8,128)(2,1)S(1)}, u32[]{:S(2)}, u32[]{:S(2)}) collective-permute-start(f16[264,512]{1,0:T(8,128)(2,1)S(1)} %concatenate.15), channel_id=1, source_target_pairs={{0,4},{2,6},{4,0},{6,2},{1,5},{3,7},{5,1},{7,3},{8,12},{10,14},{12... | collective-permute-start | bytes 811016 | tf_op jit(solution)/shard_map/ppermute | solution.py:131
  40.5 14.6 %collective-permute-start.4 = (f16[264,512]{1,0:T(8,128)(2,1)S(1)}, f16[264,512]{1,0:T(8,128)(2,1)S(1)}, u32[]{:S(2)}, u32[]{:S(2)}) collective-permute-start(f16[264,512]{1,0:T(8,128)(2,1)S(1)} %concatenate.15), channel_id=1, source_target_pairs={{0,2},{2,4},{4,6},{6,0},{1,3},{3,5},{5,7},{7,1},{8,10},{10,12},{12... | collective-permute-start | bytes 811016 | tf_op jit(solution)/shard_map/ppermute | solution.py:131
  58.8 23.5 %copy-start.1 = (bf16[1024,512]{1,0:T(8,128)(2,1)}, bf16[1024,512]{1,0:T(8,128)(2,1)S(1)}, u32[]{:S(2)}) copy-start(bf16[1024,512]{1,0:T(8,128)(2,1)S(1)} %get-tuple-element.13.refs_8_) | copy-start | bytes 3145732
  58.8 1.3 collective-permute-start.7
  58.8 33.1 %collective-permute-start.19 = (bf16[1024,512]{1,0:T(8,128)(2,1)}, bf16[1024,512]{1,0:T(8,128)(2,1)}, u32[]{:S(2)}, u32[]{:S(2)}) collective-permute-start(bf16[1024,512]{1,0:T(8,128)(2,1)} %get-tuple-element.14.refs_9_), channel_id=1, source_target_pairs={{0,1},{1,0},{2,3},{3,2},{4,5},{5,4},{6,7},{7,6},{8,9},{9,8},{10,11... | collective-permute-start | bytes 3145736 | tf_op jit(solution)/shard_map/ppermute | solution.py:135
  59.3 35.9 %collective-permute-start.18 = (bf16[1024,512]{1,0:T(8,128)(2,1)S(1)}, bf16[1024,512]{1,0:T(8,128)(2,1)S(1)}, u32[]{:S(2)}, u32[]{:S(2)}) collective-permute-start(bf16[1024,512]{1,0:T(8,128)(2,1)S(1)} %get-tuple-element.13.refs_8_), channel_id=1, source_target_pairs={{0,1},{1,0},{2,3},{3,2},{4,5},{5,4},{6,7},{7,6},{8,9},{9,8},{10,11... | collective-permute-start | bytes 3145736 | tf_op jit(solution)/shard_map/ppermute | solution.py:135
  60.8 16.5 %all-to-all-start = ((f32[8,8,512]{2,1,0:T(8,128)}), f32[8,8,512]{2,1,0:T(8,128)S(1)}, u32[]{:S(2)}, u32[]{:S(2)}) async-start(f32[8,8,512]{2,1,0:T(8,128)} %add_bitcast_fusion), calls=%async_computation | async-start | bytes 262144 | tf_op jit(solution)/shard_map/all_to_all | solution.py:126
  77.3 9.2 %collective-permute-start.10 = (f32[8,512]{1,0:T(8,128)S(1)}, f32[8,512]{1,0:T(8,128)S(1)}, u32[]{:S(2)}, u32[]{:S(2)}) collective-permute-start(f32[8,512]{1,0:T(8,128)S(1)} %reduce_sum.9), channel_id=1, source_target_pairs={{0,192},{64,128},{128,64},{192,0},{1,193},{65,129},{129,65},{193,1... | collective-permute-start | bytes 49160 | tf_op jit(solution)/shard_map/ppermute | solution.py:135
  80.3 6.2 %collective-permute-start.8 = (f32[8,512]{1,0:T(8,128)S(1)}, f32[8,512]{1,0:T(8,128)S(1)}, u32[]{:S(2)}, u32[]{:S(2)}) collective-permute-start(f32[8,512]{1,0:T(8,128)S(1)} %reduce_sum.9), channel_id=1, source_target_pairs={{0,64},{64,0},{128,192},{192,128},{1,65},{65,1},{129,193},{193,129... | collective-permute-start | bytes 49160 | tf_op jit(solution)/shard_map/ppermute | solution.py:135
  80.6 6.0 %collective-permute-start.9 = (f32[8,512]{1,0:T(8,128)S(1)}, f32[8,512]{1,0:T(8,128)S(1)}, u32[]{:S(2)}, u32[]{:S(2)}) collective-permute-start(f32[8,512]{1,0:T(8,128)S(1)} %reduce_sum.9), channel_id=1, source_target_pairs={{0,128},{64,192},{128,0},{192,64},{1,129},{65,193},{129,1},{193,65... | collective-permute-start | bytes 49160 | tf_op jit(solution)/shard_map/ppermute | solution.py:135
  87.2 12.4 %all-to-all-start.1 = ((f32[8,8,512]{2,1,0:T(8,128)}), f32[8,8,512]{2,1,0:T(8,128)S(1)}, u32[]{:S(2)}, u32[]{:S(2)}) async-start(f32[8,8,512]{2,1,0:T(8,128)} %broadcast_in_dim.2), calls=%async_computation.1 | async-start | bytes 262144 | tf_op jit(solution)/shard_map/all_to_all | solution.py:126
  99.6 46.5 %all-to-all-start.2 = ((bf16[32,32,512]{2,1,0:T(8,128)(2,1)}), bf16[32,32,512]{2,1,0:T(8,128)(2,1)S(1)}, u32[]{:S(2)}, u32[]{:S(2)}) async-start(bf16[32,32,512]{2,1,0:T(8,128)(2,1)} %bitcast.63), calls=%async_computation.2 | async-start | bytes 2097152 | tf_op jit(solution)/shard_map/all_to_all | solution.py:126
  108.7 6.3 %collective-permute-start.11 = (f32[64,512]{1,0:T(8,128)S(1)}, f32[64,512]{1,0:T(8,128)S(1)}, u32[]{:S(2)}, u32[]{:S(2)}) collective-permute-start(f32[64,512]{1,0:T(8,128)S(1)} %bitcast.56), channel_id=1, source_target_pairs={{0,2},{2,4},{4,6},{6,0},{1,3},{3,5},{5,7},{7,1},{8,10},{10,12},{12... | collective-permute-start | bytes 393224 | tf_op jit(solution)/shard_map/ppermute | solution.py:131
  108.8 8.5 %collective-permute-start.12 = (f32[64,512]{1,0:T(8,128)S(1)}, f32[64,512]{1,0:T(8,128)S(1)}, u32[]{:S(2)}, u32[]{:S(2)}) collective-permute-start(f32[64,512]{1,0:T(8,128)S(1)} %bitcast.57), channel_id=1, source_target_pairs={{0,4},{2,6},{4,0},{6,2},{1,5},{3,7},{5,1},{7,3},{8,12},{10,14},{12... | collective-permute-start | bytes 393224 | tf_op jit(solution)/shard_map/ppermute | solution.py:131
  113.0 5.0 %collective-permute-start.13 = (f32[64,512]{1,0:T(8,128)S(1)}, f32[64,512]{1,0:T(8,128)S(1)}, u32[]{:S(2)}, u32[]{:S(2)}) collective-permute-start(f32[64,512]{1,0:T(8,128)S(1)} %bitcast.58), channel_id=1, source_target_pairs={{0,6},{2,0},{4,2},{6,4},{1,7},{3,1},{5,3},{7,5},{8,14},{10,8},{12,... | collective-permute-start | bytes 393224 | tf_op jit(solution)/shard_map/ppermute | solution.py:131
  113.0 5.0 %collective-permute-start.14 = (f32[64,512]{1,0:T(8,128)S(1)}, f32[64,512]{1,0:T(8,128)S(1)}, u32[]{:S(2)}, u32[]{:S(2)}) collective-permute-start(f32[64,512]{1,0:T(8,128)S(1)} %bitcast.59), channel_id=1, source_target_pairs={{0,1},{1,0},{2,3},{3,2},{4,5},{5,4},{6,7},{7,6},{8,9},{9,8},{10,11... | collective-permute-start | bytes 393224 | tf_op jit(solution)/shard_map/ppermute | solution.py:135
  115.0 3.0 %collective-permute-start.15 = (f32[64,512]{1,0:T(8,128)S(1)}, f32[64,512]{1,0:T(8,128)S(1)}, u32[]{:S(2)}, u32[]{:S(2)}) collective-permute-start(f32[64,512]{1,0:T(8,128)S(1)} %collective-permute-done.11.refs_1_), channel_id=1, source_target_pairs={{0,1},{1,0},{2,3},{3,2},{4,5},{5,4},{6,7},{7,6},{8,9},{9,8},{10,11... | collective-permute-start | bytes 393224 | tf_op jit(solution)/shard_map/ppermute | solution.py:135
  117.4 1.3 collective-permute-start.16
  118.0 1.3 collective-permute-start.17
  (8 other events, 12.8 us)

commit v3 on v2

--- a/solution.py
+++ b/solution.py
@@ -86,17 +86,10 @@
 
     r_ref[...] = jnp.zeros_like(r_ref)
     w_ref[...] = jnp.zeros_like(w_ref)
-    def factor_block(b, _):
-        here = pl.ds(pl.multiple_of(b * NB, NB), NB)
-        upper, inv = diag_factor(s_ref[here, here])
-        r_ref[here, here] = upper
-        w_ref[here, here] = inv
-        for i in range(n):
-            pl.when(b == i)(functools.partial(after_block, i))
-        return 0
-
-    def after_block(b):
-        inv = w_ref[at(b), at(b)]
+    for b in range(n):
+        upper, inv = diag_factor(s_ref[at(b), at(b)])
+        r_ref[at(b), at(b)] = upper
+        w_ref[at(b), at(b)] = inv
         if b < n - 1:
             rest = slice(NB * (b + 1), NB * n)
             r_ref[at(b), rest] = nn(inv, s_ref[at(b), rest])
@@ -107,7 +100,6 @@
             left = tn(r_ref[0 : NB * b, at(b)], w_ref[0 : NB * b, 0 : NB * b])
             w_ref[at(b), 0 : NB * b] = -nn(inv, left)
 
-    lax.fori_loop(0, n, factor_block, 0)
 
 X, Z, Y, C = "tok_0", "tok_1", "feat_0", "feat_1"
 TOK = (X, Z)
@@ -115,6 +107,8 @@
 TAIL = 8
 F32, BF16, F16 = jnp.float32, jnp.bfloat16, jnp.float16
 VMEM = pl.BlockSpec(memory_space=pltpu.VMEM)
+ANY = pl.BlockSpec(memory_space=pl.ANY)
+HBM = pl.BlockSpec(memory_space=pltpu.HBM)
 SMEM = pl.BlockSpec(memory_space=pltpu.SMEM)
 
 
@@ -143,15 +137,21 @@
     return lax.dynamic_index_in_dim(blocks, i, 0, keepdims=False)
 
 
-def packed(values, power):
-    tail = jnp.full((TAIL, values.shape[1]), power.astype(F16))
-    return jnp.concatenate([(values * jnp.exp2(LEVEL - power)).astype(F16), tail])
+def tail_of(power, columns):
+    i = lax.broadcasted_iota(F32, (TAIL, columns), 0)
+    return jnp.exp2(jnp.floor((power - LEVEL + i) / TAIL)).astype(F16)
+
+
+def unit_of(tail):
+    rows = [tail[i : i + 1].astype(F32) for i in range(TAIL)]
+    while len(rows) > 1:
+        rows = [a * b for a, b in zip(rows[0::2], rows[1::2])]
+    return rows[0]
 
 
 def unpacked(block):
     rows = block.shape[0] - TAIL
-    power = block[rows, 0].astype(F32)
-    return block[:rows].astype(F32) * jnp.exp2(power - LEVEL), power
+    return block[:rows].astype(F32) * unit_of(block[rows:])
 
 
 def split(values):
@@ -169,6 +169,10 @@
 
 def part(i, size):
     return pl.ds(pl.multiple_of(i * size, size), size)
+
+
+def partial_kernel(place_ref, slab_ref, sketch_ref, out_ref):
+    out_ref[...] = dot_nn(slab_ref[...], sketch_ref[...])
 
 
 def share_kernel(place_ref, *refs):
@@ -191,11 +195,14 @@
 
 
 def basis_kernel(scale, place_ref, *refs):
-    mine, other = refs[0:4], refs[4:8]
-    hm_ref, lm_ref, ho_ref, lo_ref, q_ref, out_ref, uh_ref, ul_ref, s_ref, r_ref, w_ref = refs[8:]
+    mine, other, sources = refs[0:4], refs[4:8], refs[8:12]
+    q_ref, out_ref, uh_ref, ul_ref, s_ref, r_ref, w_ref, y_ref, b_ref, in_sems, out_sems = refs[12:]
     core, row = place_ref[0], place_ref[1]
     half = mine[0].shape[0]
     columns = s_ref.shape[0]
+    arriving = [pltpu.make_async_copy(sources[i], y_ref.at[i], in_sems.at[i]) for i in range(4)]
+    for copy in arriving:
+        copy.start()
     for s in range(4):
         strip = 2 * lax.rem(row + 4 - s, 4)
         s_ref[part(strip + core, half), :] = mine[s][...]
@@ -207,23 +214,47 @@
         high = u.astype(BF16)
         uh_ref[:, j : j + NB] = high
         ul_ref[:, j : j + NB] = (u - high.astype(F32)).astype(BF16)
-    rows = hm_ref.shape[0]
-    step = 256
-    for place, h_ref, l_ref in ((core, hm_ref, lm_ref), (1 - core, ho_ref, lo_ref)):
-
-        def some_rows(i, _, place=place, h_ref=h_ref, l_ref=l_ref):
-            at, out = part(i, step), part(place * (rows // step) + i, step)
-            for j in range(0, columns, 256):
-                k = j + 256
-                h, l = h_ref[at, :k], l_ref[at, :k]
-                uh, ul = uh_ref[:k, j:k], ul_ref[:k, j:k]
-                q_ref[out, j:k] = (dot_nn(h, uh) + (dot_nn(h, ul) + dot_nn(l, uh))).astype(BF16)
-            return 0
-
-        lax.fori_loop(0, rows // step, some_rows, 0)
-
-
-def image_kernel(in_ref, uh_ref, ul_ref, out_ref):
+    for copy in arriving:
+        copy.wait()
+    rows, step = y_ref.shape[1], 256
+    per = rows // step
+
+    def leaving(i):
+        which = lax.div(i, per)
+        place = jnp.where(which == 0, core, 1 - core) * per + lax.rem(i, per)
+        return pltpu.make_async_copy(b_ref.at[i], q_ref.at[part(place, step)], out_sems.at[i])
+
+    def some_rows(i, _):
+        which, at = lax.div(i, per), part(lax.rem(i, per), step)
+        for j in range(0, columns, 256):
+            k = j + 256
+            h, l = y_ref[2 * which, at, :k], y_ref[2 * which + 1, at, :k]
+            uh, ul = uh_ref[:k, j:k], ul_ref[:k, j:k]
+            b_ref[i, :, j:k] = (dot_nn(h, uh) + (dot_nn(h, ul) + dot_nn(l, uh))).astype(BF16)
+        leaving(i).start()
+        return 0
+
+    lax.fori_loop(0, 2 * per, some_rows, 0)
+    for i in range(2 * per):
+        leaving(i).wait()
+
+
+def project_kernel(place_ref, slab_ref, hm_ref, lm_ref, ho_ref, lo_ref, out_ref):
+    core, rows = place_ref[0], hm_ref.shape[0]
+    a, b = slab_ref[part(core, rows), :], slab_ref[part(1 - core, rows), :]
+    total = (dot_tn(a, hm_ref[...]) + dot_tn(b, ho_ref[...])) + (
+        dot_tn(a, lm_ref[...]) + dot_tn(b, lo_ref[...])
+    )
+    out_ref[...] = total.astype(BF16)
+
+
+def image_kernel(in_any, uh_any, ul_any, out_ref, in_ref, uh_ref, ul_ref, sems):
+    pairs = ((in_any, in_ref), (uh_any, uh_ref), (ul_any, ul_ref))
+    copies = [pltpu.make_async_copy(a, b, sems.at[i]) for i, (a, b) in enumerate(pairs)]
+    for copy in copies:
+        copy.start()
+    for copy in copies:
+        copy.wait()
     total = in_ref[0].astype(F32)
     for i in range(1, in_ref.shape[0]):
         total = total + in_ref[i].astype(F32)
@@ -238,23 +269,45 @@
     place = jnp.stack([core, row]).astype(jnp.int32)
     tokens, columns = slab.shape[0], sketch.shape[1]
     half, block, strip = tokens // 2, tokens // 8, columns // 4
-    halves = slab.reshape(2, half, slab.shape[1])
 
     def partial(which):
-        return jnp.dot(block_of(halves, which), sketch, preferred_element_type=F32)
+        tile = 256
+        first = lambda i, place: (place[0] * (half // tile) + i, 0)
+        return pl.pallas_call(
+            partial_kernel,
+            out_shape=struct((half, columns), F32),
+            grid_spec=pltpu.PrefetchScalarGridSpec(
+                num_scalar_prefetch=1,
+                grid=(half // tile,),
+                in_specs=[
+                    pl.BlockSpec((tile, slab.shape[1]), first),
+                    pl.BlockSpec(sketch.shape, lambda i, place: (0, 0)),
+                ],
+                out_specs=pl.BlockSpec((tile, columns), lambda i, place: (i, 0)),
+            ),
+            compiler_params=pltpu.CompilerParams(vmem_limit_bytes=16 << 20),
+            cost_estimate=pl.CostEstimate(
+                flops=2 * half * slab.shape[1] * columns,
+                bytes_accessed=2 * half * slab.shape[1] + 4 * half * columns,
+                transcendentals=0,
+            ),
+            name="partial",
+        )(jnp.reshape(which, (1,)).astype(jnp.int32), slab, sketch)
 
     theirs = from_partner(partial(1 - core))
-    mine = lax.optimization_barrier(partial(core))
-    pair_sum = (mine + theirs).reshape(4, block, columns)
-    power = jnp.clip(jnp.floor(jnp.log2(jnp.max(jnp.abs(pair_sum)))), -100.0, 40.0)
-    own, top = block_of(pair_sum, row), power
+    pair_sum = (partial(core) + theirs).reshape(4, block, columns)
+    power = jnp.clip(jnp.floor(jnp.log2(jnp.max(jnp.abs(pair_sum)))), 16.0 - 8 * LEVEL, 40.0)
+    lift = jnp.exp2(LEVEL - power)
+    tail = tail_of(power, columns)
+    own, top = block_of(pair_sum, row), tail
     for s in range(1, 4):
-        sent = packed(block_of(pair_sum, (row + s) % 4), power)
-        values, its_power = unpacked(shifted(sent, Y, s))
-        own, top = own + values, jnp.maximum(top, its_power)
-    message = packed(own, top + 2.0)
-    pieces = [split(unpacked(message)[0])]
-    pieces += [split(unpacked(shifted(message, Y, s))[0]) for s in range(1, 4)]
+        values = (block_of(pair_sum, (row + s) % 4) * lift).astype(F16)
+        got = shifted(jnp.concatenate([values, tail]), Y, s)
+        own, top = own + unpacked(got), jnp.maximum(top, got[block:])
+    top = jnp.where(lax.broadcasted_iota(jnp.int32, top.shape, 0) < 2, top * 2, top)
+    message = jnp.concatenate([(own / unit_of(top)).astype(F16), top])
+    pieces = [split(unpacked(message))]
+    pieces += [split(unpacked(shifted(message, Y, s))) for s in range(1, 4)]
 
     pair = struct((half, columns), BF16)
     slice_of = struct((strip // 2, columns), F32)
@@ -270,18 +323,36 @@
     strip_sum = kept + from_partner(given)
     high_other, low_other = from_partner(high_mine), from_partner(low_mine)
 
-    summed = exchange(strip_sum.reshape(8, -1, columns), Z).sum(axis=0)
+    features = slab.shape[1]
+    tile = 256
+    whole = pl.BlockSpec((half, columns), lambda i: (0, 0))
+    images = pl.pallas_call(
+        project_kernel,
+        out_shape=struct((features, columns), BF16),
+        grid=(features // tile,),
+        in_specs=[SMEM, pl.BlockSpec((tokens, tile), lambda i: (0, i))] + [whole] * 4,
+        out_specs=pl.BlockSpec((tile, columns), lambda i: (i, 0)),
+        compiler_params=pltpu.CompilerParams(vmem_limit_bytes=24 << 20),
+        cost_estimate=pl.CostEstimate(
+            flops=4 * tokens * features * columns,
+            bytes_accessed=2 * tokens * (features + 2 * columns) + 2 * features * columns,
+            transcendentals=0,
+        ),
+        name="project",
+    )(place, slab, high_mine, low_mine, high_other, low_other)
+
+    arrived = exchange(strip_sum.reshape(8, -1, columns), Z)
+    arrived, images = lax.optimization_barrier((arrived, images))
+    summed = arrived.sum(axis=0)
     summed = (summed + flipped(summed, X, 1)) + (flipped(summed, X, 2) + flipped(summed, X, 3))
     done = exchange(jnp.broadcast_to(summed[None], (8, *summed.shape)), Z).reshape(-1, columns)
 
-    def onto(which, values):
-        return dot_tn(block_of(halves, which), values)
-
-    images = onto(core, high_mine) + onto(core, low_mine)
-    images = images + (onto(1 - core, high_other) + onto(1 - core, low_other))
-    image = exchange(images.astype(BF16).reshape(32, -1, columns), TOK)
-
-    strips = [done] + [shifted(done, Y, s) for s in range(1, 4)]
+    strips = [done]
+    for s in range(1, 4):
+        strips.append(shifted(done, Y, s))
+    others = [from_partner(s) for s in strips]
+    image = exchange(images.reshape(32, -1, columns), TOK)
+
     square = struct((columns, columns), BF16)
     token_count = tokens * lax.axis_size(TOK)
     q_basis, r_scaled, upper_high, upper_low = pl.pallas_call(
@@ -289,18 +360,35 @@
         out_shape=(
             struct((tokens, columns), BF16), struct((columns, columns), F32), square, square
         ),
-        in_specs=[SMEM] + [VMEM] * 12,
-        out_specs=(VMEM,) * 4,
-        scratch_shapes=[pltpu.VMEM((columns, columns), F32)] * 3,
+        in_specs=[SMEM] + [VMEM] * 8 + [HBM] * 4,
+        out_specs=(ANY,) + (VMEM,) * 3,
+        scratch_shapes=[pltpu.VMEM((columns, columns), F32)] * 3
+        + [
+            pltpu.VMEM((4, half, columns), BF16),
+            pltpu.VMEM((8, tokens // 8, columns), BF16),
+            pltpu.SemaphoreType.DMA((4,)),
+            pltpu.SemaphoreType.DMA((8,)),
+        ],
         compiler_params=pltpu.CompilerParams(vmem_limit_bytes=24 << 20),
+        cost_estimate=pl.CostEstimate(
+            flops=20 * tokens * columns * columns,
+            bytes_accessed=16 * tokens * columns,
+            transcendentals=0,
+        ),
         name="basis",
-    )(place, *strips, *[from_partner(s) for s in strips], high_mine, low_mine, high_other, low_other)
+    )(place, *strips, *others, high_mine, low_mine, high_other, low_other)
     projected = pl.pallas_call(
         image_kernel,
         out_shape=struct((image.shape[1], columns), F32),
-        in_specs=[VMEM] * 3,
+        in_specs=[ANY] * 3,
         out_specs=VMEM,
-        compiler_params=pltpu.CompilerParams(vmem_limit_bytes=8 << 20),
+        scratch_shapes=[
+            pltpu.VMEM(image.shape, BF16),
+            pltpu.VMEM((columns, columns), BF16),
+            pltpu.VMEM((columns, columns), BF16),
+            pltpu.SemaphoreType.DMA((3,)),
+        ],
+        compiler_params=pltpu.CompilerParams(vmem_limit_bytes=12 << 20),
         name="image",
     )(image, upper_high, upper_low)
     return (q_basis, r_scaled, projected)

time: 151 us -> 140 us (0.927)
  matrix products: 22.9 us -> 0 us
  blocking collectives: 0 us -> 14.6 us
  starting transfers between devices: 41.8 us -> 30.1 us
  Pallas kernels: 27.2 us -> 36.1 us
  waiting for transfers between devices: 32.1 us -> 39 us
  between operations: 5.9 us -> 1.82 us
  local copies, waits for them, and re-layouts: 13.5 us -> 10.7 us
    dot_general x6 -> x0, matrix products: 22.9 us -> none  [the longest x4 15.9 us: dot_tn(): lax.dot_general(a, b, (((0,), (0,)), ((), ())), preferred_element_type=F32)]
    all_to_all x0 -> x1, blocking collectives: none -> 14.6 us  [exchange(): return lax.all_to_all(blocks, axis, 0, 0, tiled=True)]
    pallas_call x0 -> x3, Pallas kernels: none -> 11 us  [the longest x1 7.52 us: body(): pl.pallas_call(project_kernel, out_shape=struct((features, columns), BF16...]
    all_to_all x3 -> x2, starting transfers between devices: 22.5 us -> 13.6 us  [exchange(): return lax.all_to_all(blocks, axis, 0, 0, tiled=True)]
    ppermute x11, waiting for transfers between devices: 2.26 us -> 9.23 us  [flipped(): lax.ppermute(array, axis, [(i, i ^ bit) for i in range(lax.axis_size(axis...]
    slice x6 -> x0, local copies, waits for them, and re-layouts: 5.1 us -> none  [unpacked(): power = block[rows, 0].astype(F32)]
    unnamed x18, local copies, waits for them, and re-layouts: 6.11 us -> 10.6 us
    all_to_all x3 -> x2, waiting for transfers between devices: 3.84 us -> 0.01 us  [exchange(): return lax.all_to_all(blocks, axis, 0, 0, tiled=True)]
  transfers between devices with their start and end apart: 23 -> 22, of which waited for: 12 -> 14; matrix products, arithmetic and copies ran while one was open for 17% -> 1% of each run, Pallas kernels for 16% -> 23%
where the time goes in v3:
time: 140 us; the launch traced here: 138 us
  waiting for transfers between devices  39 us (28%)
  Pallas kernels  36.1 us (26%)
  starting transfers between devices  30.1 us (22%)
  blocking collectives  14.6 us (10%)
  local copies, waits for them, and re-layouts  10.7 us (8%)
  other arithmetic  5.27 us (4%)
  between operations  1.82 us (1%)
    ppermute x9, waiting for transfers between devices, shifted(): lax.ppermute(array, axis, [(i, (i + shift) % peers) for i in range(peers)])  29.8 us
    pallas_call x1, Pallas kernels, body(): pl.pallas_call(functools.partial(basis_kernel, 1.0 / math.sqrt(token_coun...  22.5 us
    all_to_all x1, blocking collectives, exchange(): return lax.all_to_all(blocks, axis, 0, 0, tiled=True)  14.6 us
    all_to_all x2, starting transfers between devices, exchange(): return lax.all_to_all(blocks, axis, 0, 0, tiled=True)  13.6 us
    ppermute x9, starting transfers between devices, shifted(): lax.ppermute(array, axis, [(i, (i + shift) % peers) for i in range(peers)])  11.4 us
    unnamed x18, local copies, waits for them, and re-layouts  10.6 us
    ppermute x11, waiting for transfers between devices, flipped(): lax.ppermute(array, axis, [(i, i ^ bit) for i in range(lax.axis_size(axis...  9.23 us
    pallas_call x1, Pallas kernels, body(): pl.pallas_call(project_kernel, out_shape=struct((features, columns), BF16...  7.52 us
  transfers between devices with their start and end apart: 22, of which 14 were waited for; matrix products, arithmetic and copies ran while one was open for 1% of the time, Pallas kernels for 23%

profile of v3, /device:TPU:32, one launch (start us, length us, event | category | flops | bytes accessed | tf_op | source)
XLA Modules:
  0.0 137.5 jit_solution(7838530167989152914)
XLA Ops:
  0.6 2.2 %copy-done = bf16[2048,1024]{1,0:T(8,128)(2,1)S(1)} copy-done((bf16[2048,1024]{1,0:T(8,128)(2,1)S(1)}, bf16[2048,1024]{1,0:T(8,128)(2,1)}, u32[]{:S(2)}) %copy-start) | copy-done | bytes 4194328
  4.1 1.8 %partial.3 = f32[1024,512]{1,0:T(8,128)S(1)} custom-call(s32[1]{0:T(128)} %bitcast.2.place_ref, bf16[2048,1024]{1,0:T(8,128)(2,1)S(1)} %copy-done, bf16[1024,512]{1,0:T(8,128)(2,1)S(1)} %copy-done.3), custom_call_target="tpu_custom_call" | custom-call | flops 1073741824 | bytes 4194304 | tf_op jit(solution)/shard_map/partial/pallas_call | solution.py:276
  6.0 2.2 %copy-done.1 = bf16[2048,1024]{1,0:T(8,128)(2,1)S(1)} copy-done((bf16[2048,1024]{1,0:T(8,128)(2,1)S(1)}, bf16[2048,1024]{1,0:T(8,128)(2,1)}, u32[]{:S(2)}) %copy-start.1) | copy-done | bytes 4194328
  8.2 1.8 %partial.2 = f32[1024,512]{1,0:T(8,128)S(1)} custom-call(s32[1]{0:T(128)} %bitcast.place_ref, bf16[2048,1024]{1,0:T(8,128)(2,1)S(1)} %copy-done.1, bf16[1024,512]{1,0:T(8,128)(2,1)S(1)} %copy-done.4), custom_call_target="tpu_custom_call" | custom-call | flops 1073741824 | bytes 4194304 | tf_op jit(solution)/shard_map/partial/pallas_call | solution.py:276
  10.2 2.5 %abs_reduce_fusion = (f32[]{:T(128)}, f32[1024,512]{1,0:T(8,128)S(1)}) fusion(f32[1024,512]{1,0:T(8,128)S(1)} %partial.2, f32[1024,512]{1,0:T(8,128)} %collective-permute-done), kind=kLoop, calls=%fused_computation | loop fusion | flops 1572863 | bytes 6291460 | tf_op jit(solution)/shard_map/reduce_max | solution.py:299
  16.2 1.7 %collective-permute-start.3 = (f16[264,512]{1,0:T(8,128)(2,1)S(1)}, f16[264,512]{1,0:T(8,128)(2,1)S(1)}, u32[]{:S(2)}, u32[]{:S(2)}) collective-permute-start(f16[264,512]{1,0:T(8,128)(2,1)S(1)} %get-tuple-element.37), channel_id=1, source_target_pairs={{0,6},{2,0},{4,2},{6,4},{1,7},{3,1},{5,3},{7,5},{8,14},{10,8},{12,... | collective-permute-start | bytes 811016 | tf_op jit(solution)/shard_map/ppermute | solution.py:125
  17.9 2.0 %collective-permute-start.2 = (f16[264,512]{1,0:T(8,128)(2,1)S(1)}, f16[264,512]{1,0:T(8,128)(2,1)S(1)}, u32[]{:S(2)}, u32[]{:S(2)}) collective-permute-start(f16[264,512]{1,0:T(8,128)(2,1)S(1)} %get-tuple-element.38), channel_id=1, source_target_pairs={{0,4},{2,6},{4,0},{6,2},{1,5},{3,7},{5,1},{7,3},{8,12},{10,14},{12... | collective-permute-start | bytes 811016 | tf_op jit(solution)/shard_map/ppermute | solution.py:125
  19.8 4.8 %collective-permute-done.1 = f16[264,512]{1,0:T(8,128)(2,1)S(1)} collective-permute-done((f16[264,512]{1,0:T(8,128)(2,1)}, f16[264,512]{1,0:T(8,128)(2,1)S(1)}, u32[]{:S(2)}, u32[]{:S(2)}) %collective-permute-start.1) | collective-permute-done | bytes 270368 | tf_op jit(solution)/shard_map/ppermute | solution.py:125
  25.5 6.1 %collective-permute-done.2 = f16[264,512]{1,0:T(8,128)(2,1)S(1)} collective-permute-done((f16[264,512]{1,0:T(8,128)(2,1)S(1)}, f16[264,512]{1,0:T(8,128)(2,1)S(1)}, u32[]{:S(2)}, u32[]{:S(2)}) %collective-permute-start.2) | collective-permute-done | bytes 270368 | tf_op jit(solution)/shard_map/ppermute | solution.py:125
  35.4 6.2 %collective-permute-done.6 = f16[264,512]{1,0:T(8,128)(2,1)S(1)} collective-permute-done((f16[264,512]{1,0:T(8,128)(2,1)S(1)}, f16[264,512]{1,0:T(8,128)(2,1)S(1)}, u32[]{:S(2)}, u32[]{:S(2)}) %collective-permute-start.6) | collective-permute-done | bytes 270368 | tf_op jit(solution)/shard_map/ppermute | solution.py:125
  41.7 3.1 %collective-permute-done.5 = f16[264,512]{1,0:T(8,128)(2,1)S(1)} collective-permute-done((f16[264,512]{1,0:T(8,128)(2,1)S(1)}, f16[264,512]{1,0:T(8,128)(2,1)S(1)}, u32[]{:S(2)}, u32[]{:S(2)}) %collective-permute-start.5) | collective-permute-done | bytes 270368 | tf_op jit(solution)/shard_map/ppermute | solution.py:125
  45.0 3.2 %collective-permute-done.4 = f16[264,512]{1,0:T(8,128)(2,1)S(1)} collective-permute-done((f16[264,512]{1,0:T(8,128)(2,1)S(1)}, f16[264,512]{1,0:T(8,128)(2,1)S(1)}, u32[]{:S(2)}, u32[]{:S(2)}) %collective-permute-start.4) | collective-permute-done | bytes 270368 | tf_op jit(solution)/shard_map/ppermute | solution.py:125
  50.3 3.7 %collective-permute-done.7 = f32[64,512]{1,0:T(8,128)S(1)} collective-permute-done((f32[64,512]{1,0:T(8,128)S(1)}, f32[64,512]{1,0:T(8,128)S(1)}, u32[]{:S(2)}, u32[]{:S(2)}) %collective-permute-start.7) | collective-permute-done | bytes 131104 | tf_op jit(solution)/shard_map/ppermute | solution.py:129
  54.8 8.6 %all-to-all-start = ((f32[8,8,512]{2,1,0:T(8,128)}), f32[8,8,512]{2,1,0:T(8,128)S(1)}, u32[]{:S(2)}, u32[]{:S(2)}) async-start(f32[8,8,512]{2,1,0:T(8,128)} %add_bitcast_fusion), calls=%async_computation | async-start | bytes 262144 | tf_op jit(solution)/shard_map/all_to_all | solution.py:120
  63.4 2.6 %copy-done.2 = bf16[2048,1024]{1,0:T(8,128)(2,1)S(1)} copy-done((bf16[2048,1024]{1,0:T(8,128)(2,1)S(1)}, bf16[2048,1024]{1,0:T(8,128)(2,1)}, u32[]{:S(2)}) %copy-start.2) | copy-done | bytes 4194328
  65.9 7.5 %project.1 = bf16[1024,512]{1,0:T(8,128)(2,1)} custom-call(s32[2]{0:T(128)S(1)} %pad_add_fusion.place_ref, bf16[2048,1024]{1,0:T(8,128)(2,1)S(1)} %copy-done.2, bf16[1024,512]{1,0:T(8,128)(2,1)S(1)} %get-tuple-element.15.hm_ref.refs_8_, bf16[1024,512]{1,0:T(8,128)(2,1)S(1)} %get-tuple-element.16.lm_ref.refs_9_, ...), custom_call_target="tpu_custom_call" | custom-call | flops 4294967296 | bytes 9437184 | tf_op jit(solution)/shard_map/project/pallas_call | solution.py:329
  73.5 2.8 %collective-permute-start.12 = (f32[8,512]{1,0:T(8,128)S(1)}, f32[8,512]{1,0:T(8,128)S(1)}, u32[]{:S(2)}, u32[]{:S(2)}) collective-permute-start(f32[8,512]{1,0:T(8,128)S(1)} %reduce_sum.9), channel_id=1, source_target_pairs={{0,192},{64,128},{128,64},{192,0},{1,193},{65,129},{129,65},{193,1... | collective-permute-start | bytes 49160 | tf_op jit(solution)/shard_map/ppermute | solution.py:129
  78.5 3.0 %collective-permute-done.11 = f32[8,512]{1,0:T(8,128)S(1)} collective-permute-done((f32[8,512]{1,0:T(8,128)S(1)}, f32[8,512]{1,0:T(8,128)S(1)}, u32[]{:S(2)}, u32[]{:S(2)}) %collective-permute-start.11) | collective-permute-done | bytes 16416 | tf_op jit(solution)/shard_map/ppermute | solution.py:129
  81.6 14.6 %all_to_all.15 = f32[8,8,512]{2,1,0:T(8,128)S(1)} all-to-all(f32[8,8,512]{2,1,0:T(8,128)S(1)} %broadcast_in_dim.2), channel_id=1, replica_groups=mesh['tok_0'=4,'tok_1'=8,'feat_0'=4,'feat_1'=2] {'tok_1'}, dimensions={0} | all-to-all | bytes 262144 | tf_op jit(solution)/shard_map/all_to_all | solution.py:120
  96.2 5.0 %all-to-all-start.2 = ((bf16[32,32,512]{2,1,0:T(8,128)(2,1)}), bf16[32,32,512]{2,1,0:T(8,128)(2,1)S(1)}, u32[]{:S(2)}, u32[]{:S(2)}) async-start(bf16[32,32,512]{2,1,0:T(8,128)(2,1)} %bitcast.17), calls=%async_computation.2 | async-start | bytes 2097152 | tf_op jit(solution)/shard_map/all_to_all | solution.py:120
  102.0 1.7 %collective-permute-start.14 = (f32[64,512]{1,0:T(8,128)S(1)}, f32[64,512]{1,0:T(8,128)S(1)}, u32[]{:S(2)}, u32[]{:S(2)}) collective-permute-start(f32[64,512]{1,0:T(8,128)S(1)} %bitcast.33), channel_id=1, source_target_pairs={{0,4},{2,6},{4,0},{6,2},{1,5},{3,7},{5,1},{7,3},{8,12},{10,14},{12... | collective-permute-start | bytes 393224 | tf_op jit(solution)/shard_map/ppermute | solution.py:125
  104.4 1.9 %collective-permute-done.15.refs_3_ = f32[64,512]{1,0:T(8,128)S(1)} collective-permute-done((f32[64,512]{1,0:T(8,128)S(1)}, f32[64,512]{1,0:T(8,128)S(1)}, u32[]{:S(2)}, u32[]{:S(2)}) %collective-permute-start.15) | collective-permute-done | bytes 131104 | tf_op jit(solution)/shard_map/ppermute | solution.py:125
  106.3 2.1 %collective-permute-done.14.refs_2_ = f32[64,512]{1,0:T(8,128)S(1)} collective-permute-done((f32[64,512]{1,0:T(8,128)S(1)}, f32[64,512]{1,0:T(8,128)S(1)}, u32[]{:S(2)}, u32[]{:S(2)}) %collective-permute-start.14) | collective-permute-done | bytes 131104 | tf_op jit(solution)/shard_map/ppermute | solution.py:125
  113.6 22.5 %basis.1 = (bf16[2048,512]{1,0:T(8,128)(2,1)}, f32[512,512]{1,0:T(8,128)}, bf16[512,512]{1,0:T(8,128)(2,1)S(1)}, bf16[512,512]{1,0:T(8,128)(2,1)S(1)}) custom-call(s32[2]{0:T(128)S(1)} %pad_add_fusion.place_ref, f32[64,512]{1,0:T(8,128)S(1)} %bitcast.36, f32[64,512]{1,0:T(8,128)S(1)} %collective-permute-done.13.refs_1_, ...), custom_call_target="tpu_custom_call" | custom-call | flops 10737418240 | bytes 16777216 | tf_op jit(solution)/shard_map/basis/pallas_call | solution.py:358
  (70 shorter events, 22.2 us)
Async XLA Ops:
  5.8 4.4 %collective-permute-start = (f32[1024,512]{1,0:T(8,128)S(1)}, f32[1024,512]{1,0:T(8,128)}, u32[]{:S(2)}, u32[]{:S(2)}) collective-permute-start(f32[1024,512]{1,0:T(8,128)S(1)} %partial.3), channel_id=1, source_target_pairs={{0,1},{1,0},{2,3},{3,2},{4,5},{5,4},{6,7},{7,6},{8,9},{9,8},{10,11... | collective-permute-start | bytes 6291464 | tf_op jit(solution)/shard_map/ppermute | solution.py:129
  14.6 10.1 %collective-permute-start.1 = (f16[264,512]{1,0:T(8,128)(2,1)}, f16[264,512]{1,0:T(8,128)(2,1)S(1)}, u32[]{:S(2)}, u32[]{:S(2)}) collective-permute-start(f16[264,512]{1,0:T(8,128)(2,1)} %get-tuple-element.36), channel_id=1, source_target_pairs={{0,2},{2,4},{4,6},{6,0},{1,3},{3,5},{5,7},{7,1},{8,10},{10,12},{12... | collective-permute-start | bytes 811016 | tf_op jit(solution)/shard_map/ppermute | solution.py:125
  16.2 9.4 %collective-permute-start.3 = (f16[264,512]{1,0:T(8,128)(2,1)S(1)}, f16[264,512]{1,0:T(8,128)(2,1)S(1)}, u32[]{:S(2)}, u32[]{:S(2)}) collective-permute-start(f16[264,512]{1,0:T(8,128)(2,1)S(1)} %get-tuple-element.37), channel_id=1, source_target_pairs={{0,6},{2,0},{4,2},{6,4},{1,7},{3,1},{5,3},{7,5},{8,14},{10,8},{12,... | collective-permute-start | bytes 811016 | tf_op jit(solution)/shard_map/ppermute | solution.py:125
  17.9 13.8 %collective-permute-start.2 = (f16[264,512]{1,0:T(8,128)(2,1)S(1)}, f16[264,512]{1,0:T(8,128)(2,1)S(1)}, u32[]{:S(2)}, u32[]{:S(2)}) collective-permute-start(f16[264,512]{1,0:T(8,128)(2,1)S(1)} %get-tuple-element.38), channel_id=1, source_target_pairs={{0,4},{2,6},{4,0},{6,2},{1,5},{3,7},{5,1},{7,3},{8,12},{10,14},{12... | collective-permute-start | bytes 811016 | tf_op jit(solution)/shard_map/ppermute | solution.py:125
  32.2 9.4 %collective-permute-start.6 = (f16[264,512]{1,0:T(8,128)(2,1)S(1)}, f16[264,512]{1,0:T(8,128)(2,1)S(1)}, u32[]{:S(2)}, u32[]{:S(2)}) collective-permute-start(f16[264,512]{1,0:T(8,128)(2,1)S(1)} %pad_maximum_fusion.3), channel_id=1, source_target_pairs={{0,6},{2,0},{4,2},{6,4},{1,7},{3,1},{5,3},{7,5},{8,14},{10,8},{12,... | collective-permute-start | bytes 811016 | tf_op jit(solution)/shard_map/ppermute | solution.py:125
  33.9 10.9 %collective-permute-start.5 = (f16[264,512]{1,0:T(8,128)(2,1)S(1)}, f16[264,512]{1,0:T(8,128)(2,1)S(1)}, u32[]{:S(2)}, u32[]{:S(2)}) collective-permute-start(f16[264,512]{1,0:T(8,128)(2,1)S(1)} %pad_maximum_fusion.3), channel_id=1, source_target_pairs={{0,4},{2,6},{4,0},{6,2},{1,5},{3,7},{5,1},{7,3},{8,12},{10,14},{12... | collective-permute-start | bytes 811016 | tf_op jit(solution)/shard_map/ppermute | solution.py:125
  35.4 12.8 %collective-permute-start.4 = (f16[264,512]{1,0:T(8,128)(2,1)S(1)}, f16[264,512]{1,0:T(8,128)(2,1)S(1)}, u32[]{:S(2)}, u32[]{:S(2)}) collective-permute-start(f16[264,512]{1,0:T(8,128)(2,1)S(1)} %pad_maximum_fusion.3), channel_id=1, source_target_pairs={{0,2},{2,4},{4,6},{6,0},{1,3},{3,5},{5,7},{7,1},{8,10},{10,12},{12... | collective-permute-start | bytes 811016 | tf_op jit(solution)/shard_map/ppermute | solution.py:125
  49.6 23.8 %copy-start.5 = (bf16[1024,512]{1,0:T(8,128)(2,1)}, bf16[1024,512]{1,0:T(8,128)(2,1)S(1)}, u32[]{:S(2)}) copy-start(bf16[1024,512]{1,0:T(8,128)(2,1)S(1)} %get-tuple-element.16.lm_ref.refs_9_) | copy-start | bytes 3145732
  49.7 13.7 %collective-permute-start.8 = (bf16[1024,512]{1,0:T(8,128)(2,1)S(1)}, bf16[1024,512]{1,0:T(8,128)(2,1)S(1)}, u32[]{:S(2)}, u32[]{:S(2)}) collective-permute-start(bf16[1024,512]{1,0:T(8,128)(2,1)S(1)} %get-tuple-element.15.hm_ref.refs_8_), channel_id=1, source_target_pairs={{0,1},{1,0},{2,3},{3,2},{4,5},{5,4},{6,7},{7,6},{8,9},{9,8},{10,11... | collective-permute-start | bytes 3145736 | tf_op jit(solution)/shard_map/ppermute | solution.py:129
  49.8 13.6 %collective-permute-start.9 = (bf16[1024,512]{1,0:T(8,128)(2,1)S(1)}, bf16[1024,512]{1,0:T(8,128)(2,1)}, u32[]{:S(2)}, u32[]{:S(2)}) collective-permute-start(bf16[1024,512]{1,0:T(8,128)(2,1)S(1)} %get-tuple-element.16.lm_ref.refs_9_), channel_id=1, source_target_pairs={{0,1},{1,0},{2,3},{3,2},{4,5},{5,4},{6,7},{7,6},{8,9},{9,8},{10,11... | collective-permute-start | bytes 3145736 | tf_op jit(solution)/shard_map/ppermute | solution.py:129
  50.2 3.8 %collective-permute-start.7 = (f32[64,512]{1,0:T(8,128)S(1)}, f32[64,512]{1,0:T(8,128)S(1)}, u32[]{:S(2)}, u32[]{:S(2)}) collective-permute-start(f32[64,512]{1,0:T(8,128)S(1)} %get-tuple-element.14), channel_id=1, source_target_pairs={{0,1},{1,0},{2,3},{3,2},{4,5},{5,4},{6,7},{7,6},{8,9},{9,8},{10,11... | collective-permute-start | bytes 393224 | tf_op jit(solution)/shard_map/ppermute | solution.py:129
  54.8 18.7 %all-to-all-start = ((f32[8,8,512]{2,1,0:T(8,128)}), f32[8,8,512]{2,1,0:T(8,128)S(1)}, u32[]{:S(2)}, u32[]{:S(2)}) async-start(f32[8,8,512]{2,1,0:T(8,128)} %add_bitcast_fusion), calls=%async_computation | async-start | bytes 262144 | tf_op jit(solution)/shard_map/all_to_all | solution.py:120
  63.4 10.1 %copy-start.7 = (bf16[1024,512]{1,0:T(8,128)(2,1)}, bf16[1024,512]{1,0:T(8,128)(2,1)S(1)}, u32[]{:S(2)}) copy-start(bf16[1024,512]{1,0:T(8,128)(2,1)S(1)} %collective-permute-done.8.ho_ref.refs_10_) | copy-start | bytes 3145732
  73.5 5.0 %collective-permute-start.12 = (f32[8,512]{1,0:T(8,128)S(1)}, f32[8,512]{1,0:T(8,128)S(1)}, u32[]{:S(2)}, u32[]{:S(2)}) collective-permute-start(f32[8,512]{1,0:T(8,128)S(1)} %reduce_sum.9), channel_id=1, source_target_pairs={{0,192},{64,128},{128,64},{192,0},{1,193},{65,129},{129,65},{193,1... | collective-permute-start | bytes 49160 | tf_op jit(solution)/shard_map/ppermute | solution.py:129
  76.3 5.2 %collective-permute-start.11 = (f32[8,512]{1,0:T(8,128)S(1)}, f32[8,512]{1,0:T(8,128)S(1)}, u32[]{:S(2)}, u32[]{:S(2)}) collective-permute-start(f32[8,512]{1,0:T(8,128)S(1)} %reduce_sum.9), channel_id=1, source_target_pairs={{0,128},{64,192},{128,0},{192,64},{1,129},{65,193},{129,1},{193,65... | collective-permute-start | bytes 49160 | tf_op jit(solution)/shard_map/ppermute | solution.py:129
  77.1 4.5 %collective-permute-start.10 = (f32[8,512]{1,0:T(8,128)S(1)}, f32[8,512]{1,0:T(8,128)S(1)}, u32[]{:S(2)}, u32[]{:S(2)}) collective-permute-start(f32[8,512]{1,0:T(8,128)S(1)} %reduce_sum.9), channel_id=1, source_target_pairs={{0,64},{64,0},{128,192},{192,128},{1,65},{65,1},{129,193},{193,129... | collective-permute-start | bytes 49160 | tf_op jit(solution)/shard_map/ppermute | solution.py:129
  96.2 39.9 %all-to-all-start.2 = ((bf16[32,32,512]{2,1,0:T(8,128)(2,1)}), bf16[32,32,512]{2,1,0:T(8,128)(2,1)S(1)}, u32[]{:S(2)}, u32[]{:S(2)}) async-start(bf16[32,32,512]{2,1,0:T(8,128)(2,1)} %bitcast.17), calls=%async_computation.2 | async-start | bytes 2097152 | tf_op jit(solution)/shard_map/all_to_all | solution.py:120
  101.3 5.0 %collective-permute-start.15 = (f32[64,512]{1,0:T(8,128)S(1)}, f32[64,512]{1,0:T(8,128)S(1)}, u32[]{:S(2)}, u32[]{:S(2)}) collective-permute-start(f32[64,512]{1,0:T(8,128)S(1)} %bitcast.32), channel_id=1, source_target_pairs={{0,6},{2,0},{4,2},{6,4},{1,7},{3,1},{5,3},{7,5},{8,14},{10,8},{12,... | collective-permute-start | bytes 393224 | tf_op jit(solution)/shard_map/ppermute | solution.py:125
  102.0 6.5 %collective-permute-start.14 = (f32[64,512]{1,0:T(8,128)S(1)}, f32[64,512]{1,0:T(8,128)S(1)}, u32[]{:S(2)}, u32[]{:S(2)}) collective-permute-start(f32[64,512]{1,0:T(8,128)S(1)} %bitcast.33), channel_id=1, source_target_pairs={{0,4},{2,6},{4,0},{6,2},{1,5},{3,7},{5,1},{7,3},{8,12},{10,14},{12... | collective-permute-start | bytes 393224 | tf_op jit(solution)/shard_map/ppermute | solution.py:125
  103.6 6.2 %collective-permute-start.13 = (f32[64,512]{1,0:T(8,128)S(1)}, f32[64,512]{1,0:T(8,128)S(1)}, u32[]{:S(2)}, u32[]{:S(2)}) collective-permute-start(f32[64,512]{1,0:T(8,128)S(1)} %bitcast.34), channel_id=1, source_target_pairs={{0,2},{2,4},{4,6},{6,0},{1,3},{3,5},{5,7},{7,1},{8,10},{10,12},{12... | collective-permute-start | bytes 393224 | tf_op jit(solution)/shard_map/ppermute | solution.py:125
  104.4 5.4 %collective-permute-start.16 = (f32[64,512]{1,0:T(8,128)S(1)}, f32[64,512]{1,0:T(8,128)S(1)}, u32[]{:S(2)}, u32[]{:S(2)}) collective-permute-start(f32[64,512]{1,0:T(8,128)S(1)} %bitcast.35), channel_id=1, source_target_pairs={{0,1},{1,0},{2,3},{3,2},{4,5},{5,4},{6,7},{7,6},{8,9},{9,8},{10,11... | collective-permute-start | bytes 393224 | tf_op jit(solution)/shard_map/ppermute | solution.py:129
  106.3 3.5 %collective-permute-start.19 = (f32[64,512]{1,0:T(8,128)S(1)}, f32[64,512]{1,0:T(8,128)S(1)}, u32[]{:S(2)}, u32[]{:S(2)}) collective-permute-start(f32[64,512]{1,0:T(8,128)S(1)} %collective-permute-done.15.refs_3_), channel_id=1, source_target_pairs={{0,1},{1,0},{2,3},{3,2},{4,5},{5,4},{6,7},{7,6},{8,9},{9,8},{10,11... | collective-permute-start | bytes 393224 | tf_op jit(solution)/shard_map/ppermute | solution.py:129
  108.4 1.4 %collective-permute-start.18 = (f32[64,512]{1,0:T(8,128)S(1)}, f32[64,512]{1,0:T(8,128)S(1)}, u32[]{:S(2)}, u32[]{:S(2)}) collective-permute-start(f32[64,512]{1,0:T(8,128)S(1)} %collective-permute-done.14.refs_2_), channel_id=1, source_target_pairs={{0,1},{1,0},{2,3},{3,2},{4,5},{5,4},{6,7},{7,6},{8,9},{9,8},{10,11... | collective-permute-start | bytes 393224 | tf_op jit(solution)/shard_map/ppermute | solution.py:129
  109.8 1.3 collective-permute-start.17
  (7 other events, 12.5 us)

commit v4 on v3

--- a/solution.py
+++ b/solution.py
@@ -105,6 +105,7 @@
 TOK = (X, Z)
 LEVEL = 14.0
 TAIL = 8
+ROOMY = 56 << 20
 F32, BF16, F16 = jnp.float32, jnp.bfloat16, jnp.float16
 VMEM = pl.BlockSpec(memory_space=pltpu.VMEM)
 ANY = pl.BlockSpec(memory_space=pl.ANY)
@@ -171,8 +172,11 @@
     return pl.ds(pl.multiple_of(i * size, size), size)
 
 
-def partial_kernel(place_ref, slab_ref, sketch_ref, out_ref):
-    out_ref[...] = dot_nn(slab_ref[...], sketch_ref[...])
+def partial_kernel(place_ref, slab_ref, sketch_ref, out_ref, top_ref):
+    product = dot_nn(slab_ref[...], sketch_ref[...])
+    out_ref[...] = product
+    top = jnp.max(jnp.max(jnp.abs(product), axis=0, keepdims=True), axis=1, keepdims=True)
+    top_ref[...] = jnp.broadcast_to(top, top_ref.shape)
 
 
 def share_kernel(place_ref, *refs):
@@ -196,24 +200,33 @@
 
 def basis_kernel(scale, place_ref, *refs):
     mine, other, sources = refs[0:4], refs[4:8], refs[8:12]
-    q_ref, out_ref, uh_ref, ul_ref, s_ref, r_ref, w_ref, y_ref, b_ref, in_sems, out_sems = refs[12:]
+    q_ref, r_any, uh_any, ul_any = refs[12:16]
+    s_ref, r_ref, w_ref, uh_ref, ul_ref, y_ref, b_ref, strip_sems, in_sems, small_sems, out_sems = refs[16:]
     core, row = place_ref[0], place_ref[1]
     half = mine[0].shape[0]
     columns = s_ref.shape[0]
-    arriving = [pltpu.make_async_copy(sources[i], y_ref.at[i], in_sems.at[i]) for i in range(4)]
-    for copy in arriving:
-        copy.start()
+    strips = []
     for s in range(4):
         strip = 2 * lax.rem(row + 4 - s, 4)
-        s_ref[part(strip + core, half), :] = mine[s][...]
-        s_ref[part(strip + 1 - core, half), :] = other[s][...]
+        for ref, side in ((mine[s], core), (other[s], 1 - core)):
+            there = s_ref.at[part(strip + side, half)]
+            strips.append(pltpu.make_async_copy(ref, there, strip_sems.at[len(strips)]))
+    arriving = [pltpu.make_async_copy(sources[i], y_ref.at[i], in_sems.at[i]) for i in range(4)]
+    for copy in strips + arriving:
+        copy.start()
+    for copy in strips:
+        copy.wait()
     factor_in_place(s_ref, r_ref, w_ref)
-    out_ref[...] = r_ref[...] * scale
+    r_ref[...] = r_ref[...] * scale
     for j in range(0, columns, NB):
         u = w_ref[j : j + NB, :].T
         high = u.astype(BF16)
         uh_ref[:, j : j + NB] = high
         ul_ref[:, j : j + NB] = (u - high.astype(F32)).astype(BF16)
+    pairs = ((r_ref, r_any), (uh_ref, uh_any), (ul_ref, ul_any))
+    small = [pltpu.make_async_copy(a, b, small_sems.at[i]) for i, (a, b) in enumerate(pairs)]
+    for copy in small:
+        copy.start()
     for copy in arriving:
         copy.wait()
     rows, step = y_ref.shape[1], 256
@@ -237,9 +250,12 @@
     lax.fori_loop(0, 2 * per, some_rows, 0)
     for i in range(2 * per):
         leaving(i).wait()
-
-
-def project_kernel(place_ref, slab_ref, hm_ref, lm_ref, ho_ref, lo_ref, out_ref):
+    for copy in small:
+        copy.wait()
+
+
+def project_kernel(place_ref, slab_ref, hm_ref, lm_ref, ho_ref, lo_ref, *refs):
+    out_ref = refs[-1]
     core, rows = place_ref[0], hm_ref.shape[0]
     a, b = slab_ref[part(core, rows), :], slab_ref[part(1 - core, rows), :]
     total = (dot_tn(a, hm_ref[...]) + dot_tn(b, ho_ref[...])) + (
@@ -273,19 +289,23 @@
     def partial(which):
         tile = 256
         first = lambda i, place: (place[0] * (half // tile) + i, 0)
+        steps = half // tile
         return pl.pallas_call(
             partial_kernel,
-            out_shape=struct((half, columns), F32),
+            out_shape=(struct((half, columns), F32), struct((8 * steps, 128), F32)),
             grid_spec=pltpu.PrefetchScalarGridSpec(
                 num_scalar_prefetch=1,
-                grid=(half // tile,),
+                grid=(steps,),
                 in_specs=[
                     pl.BlockSpec((tile, slab.shape[1]), first),
                     pl.BlockSpec(sketch.shape, lambda i, place: (0, 0)),
                 ],
-                out_specs=pl.BlockSpec((tile, columns), lambda i, place: (i, 0)),
+                out_specs=(
+                    pl.BlockSpec((tile, columns), lambda i, place: (i, 0)),
+                    pl.BlockSpec((8, 128), lambda i, place: (i, 0)),
+                ),
             ),
-            compiler_params=pltpu.CompilerParams(vmem_limit_bytes=16 << 20),
+            compiler_params=pltpu.CompilerParams(vmem_limit_bytes=ROOMY),
             cost_estimate=pl.CostEstimate(
                 flops=2 * half * slab.shape[1] * columns,
                 bytes_accessed=2 * half * slab.shape[1] + 4 * half * columns,
@@ -294,14 +314,21 @@
             name="partial",
         )(jnp.reshape(which, (1,)).astype(jnp.int32), slab, sketch)
 
-    theirs = from_partner(partial(1 - core))
-    pair_sum = (partial(core) + theirs).reshape(4, block, columns)
-    power = jnp.clip(jnp.floor(jnp.log2(jnp.max(jnp.abs(pair_sum)))), 16.0 - 8 * LEVEL, 40.0)
+    given, given_top = partial(1 - core)
+    theirs, theirs_top = from_partner(given), from_partner(given_top)
+    mine, mine_top = partial(core)
+    mine, theirs = mine.reshape(4, block, columns), theirs.reshape(4, block, columns)
+    top = jnp.max(mine_top) + jnp.max(theirs_top)
+    power = jnp.clip(jnp.floor(jnp.log2(top)), 16.0 - 8 * LEVEL, 40.0)
     lift = jnp.exp2(LEVEL - power)
     tail = tail_of(power, columns)
-    own, top = block_of(pair_sum, row), tail
+
+    def pair_sum(i):
+        return block_of(mine, i) + block_of(theirs, i)
+
+    own, top = pair_sum(row), tail
     for s in range(1, 4):
-        values = (block_of(pair_sum, (row + s) % 4) * lift).astype(F16)
+        values = (pair_sum((row + s) % 4) * lift).astype(F16)
         got = shifted(jnp.concatenate([values, tail]), Y, s)
         own, top = own + unpacked(got), jnp.maximum(top, got[block:])
     top = jnp.where(lax.broadcasted_iota(jnp.int32, top.shape, 0) < 2, top * 2, top)
@@ -321,31 +348,41 @@
         name="share",
     )(place, *[p[0] for p in pieces], *[p[1] for p in pieces])
     strip_sum = kept + from_partner(given)
+    high_mine, low_mine, strip_sum = lax.optimization_barrier((high_mine, low_mine, strip_sum))
     high_other, low_other = from_partner(high_mine), from_partner(low_mine)
 
     features = slab.shape[1]
     tile = 256
-    whole = pl.BlockSpec((half, columns), lambda i: (0, 0))
-    images = pl.pallas_call(
-        project_kernel,
-        out_shape=struct((features, columns), BF16),
-        grid=(features // tile,),
-        in_specs=[SMEM, pl.BlockSpec((tokens, tile), lambda i: (0, i))] + [whole] * 4,
-        out_specs=pl.BlockSpec((tile, columns), lambda i: (i, 0)),
-        compiler_params=pltpu.CompilerParams(vmem_limit_bytes=24 << 20),
-        cost_estimate=pl.CostEstimate(
-            flops=4 * tokens * features * columns,
-            bytes_accessed=2 * tokens * (features + 2 * columns) + 2 * features * columns,
-            transcendentals=0,
-        ),
-        name="project",
-    )(place, slab, high_mine, low_mine, high_other, low_other)
+
+    def project(first, images):
+        steps = features // tile // 2
+        whole = pl.BlockSpec((half, columns), lambda i: (0, 0))
+        return pl.pallas_call(
+            project_kernel,
+            out_shape=struct((features, columns), BF16),
+            grid=(steps,),
+            in_specs=[SMEM, pl.BlockSpec((tokens, tile), lambda i: (0, first * steps + i))]
+            + [whole] * 4
+            + [ANY] * len(images),
+            out_specs=pl.BlockSpec((tile, columns), lambda i: (first * steps + i, 0)),
+            input_output_aliases={6: 0} if images else {},
+            compiler_params=pltpu.CompilerParams(vmem_limit_bytes=ROOMY),
+            cost_estimate=pl.CostEstimate(
+                flops=2 * tokens * features * columns,
+                bytes_accessed=tokens * (features + 4 * columns) + features * columns,
+                transcendentals=0,
+            ),
+        )(place, slab, high_mine, low_mine, high_other, low_other, *images)
 
     arrived = exchange(strip_sum.reshape(8, -1, columns), Z)
+    images = project(0, ())
     arrived, images = lax.optimization_barrier((arrived, images))
     summed = arrived.sum(axis=0)
     summed = (summed + flipped(summed, X, 1)) + (flipped(summed, X, 2) + flipped(summed, X, 3))
-    done = exchange(jnp.broadcast_to(summed[None], (8, *summed.shape)), Z).reshape(-1, columns)
+    done = exchange(jnp.broadcast_to(summed[None], (8, *summed.shape)), Z)
+    images = project(1, (images,))
+    done, images = lax.optimization_barrier((done, images))
+    done = done.reshape(-1, columns)
 
     strips = [done]
     for s in range(1, 4):
@@ -360,16 +397,19 @@
         out_shape=(
             struct((tokens, columns), BF16), struct((columns, columns), F32), square, square
         ),
-        in_specs=[SMEM] + [VMEM] * 8 + [HBM] * 4,
-        out_specs=(ANY,) + (VMEM,) * 3,
+        in_specs=[SMEM] + [ANY] * 12,
+        out_specs=(ANY,) * 4,
         scratch_shapes=[pltpu.VMEM((columns, columns), F32)] * 3
+        + [pltpu.VMEM((columns, columns), BF16)] * 2
         + [
             pltpu.VMEM((4, half, columns), BF16),
             pltpu.VMEM((8, tokens // 8, columns), BF16),
+            pltpu.SemaphoreType.DMA((8,)),
             pltpu.SemaphoreType.DMA((4,)),
+            pltpu.SemaphoreType.DMA((3,)),
             pltpu.SemaphoreType.DMA((8,)),
         ],
-        compiler_params=pltpu.CompilerParams(vmem_limit_bytes=24 << 20),
+        compiler_params=pltpu.CompilerParams(vmem_limit_bytes=ROOMY),
         cost_estimate=pl.CostEstimate(
             flops=20 * tokens * columns * columns,
             bytes_accessed=16 * tokens * columns,
@@ -388,7 +428,7 @@
             pltpu.VMEM((columns, columns), BF16),
             pltpu.SemaphoreType.DMA((3,)),
         ],
-        compiler_params=pltpu.CompilerParams(vmem_limit_bytes=12 << 20),
+        compiler_params=pltpu.CompilerParams(vmem_limit_bytes=ROOMY),
         name="image",
     )(image, upper_high, upper_low)
     return (q_basis, r_scaled, projected)

time: 140 us -> 141 us (level)
  blocking collectives: 14.6 us -> 0 us
  Pallas kernels: 36.1 us -> 48.2 us
  starting transfers between devices: 30.1 us -> 38.4 us
  local copies, waits for them, and re-layouts: 10.7 us -> 3.36 us
  other arithmetic: 5.27 us -> 7.37 us
    all_to_all x1 -> x0, blocking collectives: 14.6 us -> none  [exchange(): return lax.all_to_all(blocks, axis, 0, 0, tiled=True)]
    pallas_call x3 -> x4, Pallas kernels: 11 us -> 21.5 us  [the longest x2 11.6 us: project(): pl.pallas_call(project_kernel, out_shape=struct((features, columns), BF16...]
    all_to_all x2 -> x3, starting transfers between devices: 13.6 us -> 21.7 us  [exchange(): return lax.all_to_all(blocks, axis, 0, 0, tiled=True)]
    unnamed x18 -> x26, local copies, waits for them, and re-layouts: 10.6 us -> 2.62 us
    all_to_all x2 -> x3, waiting for transfers between devices: 0.01 us -> 2.95 us  [exchange(): return lax.all_to_all(blocks, axis, 0, 0, tiled=True)]
    ppermute x11 -> x12, waiting for transfers between devices: 9.23 us -> 6.57 us  [flipped(): lax.ppermute(array, axis, [(i, i ^ bit) for i in range(lax.axis_size(axis...]
    convert_element_type x1, other arithmetic: 0.21 us -> 1.77 us  [body(): values = (pair_sum((row + s) % 4) * lift).astype(F16)]
    ppermute x11 -> x12, starting transfers between devices: 4.98 us -> 5.3 us  [flipped(): lax.ppermute(array, axis, [(i, i ^ bit) for i in range(lax.axis_size(axis...]
  transfers between devices with their start and end apart: 22 -> 24, of which waited for: 14 -> 15; matrix products, arithmetic and copies ran while one was open for 1% -> 2% of each run, Pallas kernels for 23% -> 28%
where the time goes in v4:
time: 141 us; the launch traced here: 139 us
  Pallas kernels  48.2 us (34%)
  waiting for transfers between devices  38.9 us (28%)
  starting transfers between devices  38.4 us (27%)
  other arithmetic  7.37 us (5%)
  local copies, waits for them, and re-layouts  3.36 us (2%)
  between operations  2.46 us (2%)
    ppermute x9, waiting for transfers between devices, shifted(): lax.ppermute(array, axis, [(i, (i + shift) % peers) for i in range(peers)])  29.4 us
    pallas_call x1, Pallas kernels, body(): pl.pallas_call(functools.partial(basis_kernel, 1.0 / math.sqrt(token_coun...  22.8 us
    all_to_all x3, starting transfers between devices, exchange(): return lax.all_to_all(blocks, axis, 0, 0, tiled=True)  21.7 us
    pallas_call x2, Pallas kernels, project(): pl.pallas_call(project_kernel, out_shape=struct((features, columns), BF16...  11.6 us
    ppermute x9, starting transfers between devices, shifted(): lax.ppermute(array, axis, [(i, (i + shift) % peers) for i in range(peers)])  11.5 us
    pallas_call x2, Pallas kernels, partial(): pl.pallas_call(partial_kernel, out_shape=(struct((half, columns), F32), s...  9.89 us
    ppermute x12, waiting for transfers between devices, flipped(): lax.ppermute(array, axis, [(i, i ^ bit) for i in range(lax.axis_size(axis...  6.57 us
    ppermute x12, starting transfers between devices, flipped(): lax.ppermute(array, axis, [(i, i ^ bit) for i in range(lax.axis_size(axis...  5.3 us
  transfers between devices with their start and end apart: 24, of which 15 were waited for; matrix products, arithmetic and copies ran while one was open for 2% of the time, Pallas kernels for 28%

profile of v4, /device:TPU:32, one launch (start us, length us, event | category | flops | bytes accessed | tf_op | source)
XLA Modules:
  0.0 138.7 jit_solution(6134573436300871547)
XLA Ops:
  0.6 5.0 %partial.3 = (f32[1024,512]{1,0:T(8,128)}, f32[32,128]{1,0:T(8,128)}) custom-call(s32[1]{0:T(128)} %bitcast.3.place_ref, bf16[2048,1024]{1,0:T(8,128)(2,1)} %slab_ref.7, bf16[1024,512]{1,0:T(8,128)(2,1)} %sketch_ref.3), custom_call_target="tpu_custom_call" | custom-call | flops 1073741824 | bytes 4194304 | tf_op jit(solution)/shard_map/partial/pallas_call | solution.py:293
  6.1 4.9 %partial.2 = (f32[1024,512]{1,0:T(8,128)}, f32[32,128]{1,0:T(8,128)}) custom-call(s32[1]{0:T(128)} %bitcast.place_ref, bf16[2048,1024]{1,0:T(8,128)(2,1)} %slab_ref.7, bf16[1024,512]{1,0:T(8,128)(2,1)} %sketch_ref.3), custom_call_target="tpu_custom_call" | custom-call | flops 1073741824 | bytes 4194304 | tf_op jit(solution)/shard_map/partial/pallas_call | solution.py:293
  14.4 1.8 %fusion.8 = (f16[256,512]{1,0:T(8,128)(2,1)S(1)}, f16[256,512]{1,0:T(8,128)(2,1)S(1)}, f16[256,512]{1,0:T(8,128)(2,1)S(1)}) fusion(f32[4,256,512]{2,1,0:T(8,128)S(1)} %bitcast.33, s32[]{:T(128)S(6)} %select_n.38, f32[4,256,512]{2,1,0:T(8,128)} %bitcast.35, f32[]{:T(128)S(6)} %exp2.18, s32[]{:T(128)S(6)} %select_n.42, s32[]{:T(128)S(6)} %select_n.40), kind=kLoop, calls=%fused_computation.28 | loop fusion | flops 1179648 | bytes 3932176 | tf_op jit(solution)/shard_map/convert_element_type | solution.py:331
  18.7 1.7 %collective-permute-start.4 = (f16[264,512]{1,0:T(8,128)(2,1)S(1)}, f16[264,512]{1,0:T(8,128)(2,1)S(1)}, u32[]{:S(2)}, u32[]{:S(2)}) collective-permute-start(f16[264,512]{1,0:T(8,128)(2,1)S(1)} %get-tuple-element.53), channel_id=1, source_target_pairs={{0,6},{2,0},{4,2},{6,4},{1,7},{3,1},{5,3},{7,5},{8,14},{10,8},{12,... | collective-permute-start | bytes 811016 | tf_op jit(solution)/shard_map/ppermute | solution.py:126
  20.4 2.0 %collective-permute-start.3 = (f16[264,512]{1,0:T(8,128)(2,1)S(1)}, f16[264,512]{1,0:T(8,128)(2,1)S(1)}, u32[]{:S(2)}, u32[]{:S(2)}) collective-permute-start(f16[264,512]{1,0:T(8,128)(2,1)S(1)} %get-tuple-element.54), channel_id=1, source_target_pairs={{0,4},{2,6},{4,0},{6,2},{1,5},{3,7},{5,1},{7,3},{8,12},{10,14},{12... | collective-permute-start | bytes 811016 | tf_op jit(solution)/shard_map/ppermute | solution.py:126
  22.4 4.6 %collective-permute-done.2 = f16[264,512]{1,0:T(8,128)(2,1)S(1)} collective-permute-done((f16[264,512]{1,0:T(8,128)(2,1)}, f16[264,512]{1,0:T(8,128)(2,1)S(1)}, u32[]{:S(2)}, u32[]{:S(2)}) %collective-permute-start.2) | collective-permute-done | bytes 270368 | tf_op jit(solution)/shard_map/ppermute | solution.py:126
  28.1 5.9 %collective-permute-done.3 = f16[264,512]{1,0:T(8,128)(2,1)S(1)} collective-permute-done((f16[264,512]{1,0:T(8,128)(2,1)S(1)}, f16[264,512]{1,0:T(8,128)(2,1)S(1)}, u32[]{:S(2)}, u32[]{:S(2)}) %collective-permute-start.3) | collective-permute-done | bytes 270368 | tf_op jit(solution)/shard_map/ppermute | solution.py:126
  35.6 1.6 %collective-permute-start.7 = (f16[264,512]{1,0:T(8,128)(2,1)S(1)}, f16[264,512]{1,0:T(8,128)(2,1)S(1)}, u32[]{:S(2)}, u32[]{:S(2)}) collective-permute-start(f16[264,512]{1,0:T(8,128)(2,1)S(1)} %pad_maximum_fusion.3), channel_id=1, source_target_pairs={{0,6},{2,0},{4,2},{6,4},{1,7},{3,1},{5,3},{7,5},{8,14},{10,8},{12,... | collective-permute-start | bytes 811016 | tf_op jit(solution)/shard_map/ppermute | solution.py:126
  38.8 6.2 %collective-permute-done.7 = f16[264,512]{1,0:T(8,128)(2,1)S(1)} collective-permute-done((f16[264,512]{1,0:T(8,128)(2,1)S(1)}, f16[264,512]{1,0:T(8,128)(2,1)S(1)}, u32[]{:S(2)}, u32[]{:S(2)}) %collective-permute-start.7) | collective-permute-done | bytes 270368 | tf_op jit(solution)/shard_map/ppermute | solution.py:126
  45.1 3.1 %collective-permute-done.6 = f16[264,512]{1,0:T(8,128)(2,1)S(1)} collective-permute-done((f16[264,512]{1,0:T(8,128)(2,1)S(1)}, f16[264,512]{1,0:T(8,128)(2,1)S(1)}, u32[]{:S(2)}, u32[]{:S(2)}) %collective-permute-start.6) | collective-permute-done | bytes 270368 | tf_op jit(solution)/shard_map/ppermute | solution.py:126
  48.4 3.0 %collective-permute-done.5 = f16[264,512]{1,0:T(8,128)(2,1)S(1)} collective-permute-done((f16[264,512]{1,0:T(8,128)(2,1)S(1)}, f16[264,512]{1,0:T(8,128)(2,1)S(1)}, u32[]{:S(2)}, u32[]{:S(2)}) %collective-permute-start.5) | collective-permute-done | bytes 270368 | tf_op jit(solution)/shard_map/ppermute | solution.py:126
  55.5 8.6 %all-to-all-start = ((f32[8,8,512]{2,1,0:T(8,128)}), f32[8,8,512]{2,1,0:T(8,128)S(1)}, u32[]{:S(2)}, u32[]{:S(2)}) async-start(f32[8,8,512]{2,1,0:T(8,128)} %bitcast.16), calls=%async_computation | async-start | bytes 262144 | tf_op jit(solution)/shard_map/all_to_all | solution.py:121
  65.1 5.8 %shard_map.49.refs_0_ = bf16[1024,512]{1,0:T(8,128)(2,1)} custom-call(s32[2]{0:T(128)} %copy-done.2, bf16[2048,1024]{1,0:T(8,128)(2,1)} %slab_ref.7, bf16[1024,512]{1,0:T(8,128)(2,1)} %copy-done, bf16[1024,512]{1,0:T(8,128)(2,1)} %copy-done.1, bf16[1024,512]{1,0:T(8,128)(2,1)} %copy-done.4, bf16[1024,512]{1,0:T(8,128)(2,1)} %collective-permute-done.10.lo_ref.refs_11_), custom_call_target="tpu_custom_call" | custom-call | flops 2147483648 | bytes 6815744 | tf_op jit(solution)/shard_map/pallas_call | solution.py:360
  72.0 2.9 %collective-permute-start.13 = (f32[8,512]{1,0:T(8,128)S(1)}, f32[8,512]{1,0:T(8,128)S(1)}, u32[]{:S(2)}, u32[]{:S(2)}) collective-permute-start(f32[8,512]{1,0:T(8,128)S(1)} %reduce_sum.9), channel_id=1, source_target_pairs={{0,192},{64,128},{128,64},{192,0},{1,193},{65,129},{129,65},{193,1... | collective-permute-start | bytes 49160 | tf_op jit(solution)/shard_map/ppermute | solution.py:130
  77.0 3.1 %collective-permute-done.12 = f32[8,512]{1,0:T(8,128)S(1)} collective-permute-done((f32[8,512]{1,0:T(8,128)S(1)}, f32[8,512]{1,0:T(8,128)S(1)}, u32[]{:S(2)}, u32[]{:S(2)}) %collective-permute-start.12) | collective-permute-done | bytes 16416 | tf_op jit(solution)/shard_map/ppermute | solution.py:130
  80.8 6.1 %all-to-all-start.1 = ((f32[8,8,512]{2,1,0:T(8,128)}), f32[8,8,512]{2,1,0:T(8,128)S(1)}, u32[]{:S(2)}, u32[]{:S(2)}) async-start(f32[8,8,512]{2,1,0:T(8,128)} %broadcast_in_dim.2), calls=%async_computation.1 | async-start | bytes 262144 | tf_op jit(solution)/shard_map/all_to_all | solution.py:121
  86.9 5.8 %shard_map.50 = bf16[1024,512]{1,0:T(8,128)(2,1)} custom-call(s32[2]{0:T(128)} %copy-done.2, bf16[2048,1024]{1,0:T(8,128)(2,1)} %slab_ref.7, bf16[1024,512]{1,0:T(8,128)(2,1)} %copy-done, bf16[1024,512]{1,0:T(8,128)(2,1)} %copy-done.1, bf16[1024,512]{1,0:T(8,128)(2,1)} %copy-done.4, ...), custom_call_target="tpu_custom_call", output_to_operand_aliasing={{}: (6, {})} | custom-call | flops 2147483648 | bytes 6815744 | tf_op jit(solution)/shard_map/pallas_call | solution.py:360
  92.7 1.8 %all-to-all-done.1 = f32[8,8,512]{2,1,0:T(8,128)S(1)} async-done(((f32[8,8,512]{2,1,0:T(8,128)}), f32[8,8,512]{2,1,0:T(8,128)S(1)}, u32[]{:S(2)}, u32[]{:S(2)}) %all-to-all-start.1) | async-done | bytes 131104 | tf_op jit(solution)/shard_map/all_to_all | solution.py:121
  94.5 7.0 %all-to-all-start.2 = ((bf16[32,32,512]{2,1,0:T(8,128)(2,1)}), bf16[32,32,512]{2,1,0:T(8,128)(2,1)S(1)}, u32[]{:S(2)}, u32[]{:S(2)}) async-start(bf16[32,32,512]{2,1,0:T(8,128)(2,1)} %bitcast.32), calls=%async_computation.2 | async-start | bytes 2097152 | tf_op jit(solution)/shard_map/all_to_all | solution.py:121
  102.2 1.6 %collective-permute-start.15 = (f32[64,512]{1,0:T(8,128)S(1)}, f32[64,512]{1,0:T(8,128)S(1)}, u32[]{:S(2)}, u32[]{:S(2)}) collective-permute-start(f32[64,512]{1,0:T(8,128)S(1)} %bitcast.38), channel_id=1, source_target_pairs={{0,4},{2,6},{4,0},{6,2},{1,5},{3,7},{5,1},{7,3},{8,12},{10,14},{12... | collective-permute-start | bytes 393224 | tf_op jit(solution)/shard_map/ppermute | solution.py:126
  104.7 1.9 %collective-permute-done.16.refs_3_ = f32[64,512]{1,0:T(8,128)S(1)} collective-permute-done((f32[64,512]{1,0:T(8,128)S(1)}, f32[64,512]{1,0:T(8,128)S(1)}, u32[]{:S(2)}, u32[]{:S(2)}) %collective-permute-start.16) | collective-permute-done | bytes 131104 | tf_op jit(solution)/shard_map/ppermute | solution.py:126
  106.6 2.1 %collective-permute-done.15.refs_2_ = f32[64,512]{1,0:T(8,128)S(1)} collective-permute-done((f32[64,512]{1,0:T(8,128)S(1)}, f32[64,512]{1,0:T(8,128)S(1)}, u32[]{:S(2)}, u32[]{:S(2)}) %collective-permute-start.15) | collective-permute-done | bytes 131104 | tf_op jit(solution)/shard_map/ppermute | solution.py:126
  112.1 22.8 %basis.1 = (bf16[2048,512]{1,0:T(8,128)(2,1)}, f32[512,512]{1,0:T(8,128)}, bf16[512,512]{1,0:T(8,128)(2,1)}, bf16[512,512]{1,0:T(8,128)(2,1)}) custom-call(s32[2]{0:T(128)} %copy-done.2, f32[64,512]{1,0:T(8,128)} %bitcast.41, f32[64,512]{1,0:T(8,128)} %copy-done.8, f32[64,512]{1,0:T(8,128)} %copy-done.7, f32[64,512]{1,0:T(8,128)} %copy-done.6, ...), custom_call_target="tpu_custom_call" | custom-call | flops 10737418240 | bytes 16777216 | tf_op jit(solution)/shard_map/basis/pallas_call | solution.py:395
  136.0 2.6 %image.1 = f32[32,512]{1,0:T(8,128)} custom-call(bf16[32,32,512]{2,1,0:T(8,128)(2,1)} %copy-done.3, bf16[512,512]{1,0:T(8,128)(2,1)} %get-tuple-element.39.uh_any, bf16[512,512]{1,0:T(8,128)(2,1)} %get-tuple-element.40.ul_any), custom_call_target="tpu_custom_call" | custom-call | tf_op jit(solution)/shard_map/image/pallas_call | solution.py:420
  (83 shorter events, 24.3 us)
Async XLA Ops:
  5.6 8.8 %collective-permute-start = (f32[1024,512]{1,0:T(8,128)}, f32[1024,512]{1,0:T(8,128)S(1)}, u32[]{:S(2)}, u32[]{:S(2)}) collective-permute-start(f32[1024,512]{1,0:T(8,128)} %get-tuple-element.23), channel_id=1, source_target_pairs={{0,1},{1,0},{2,3},{3,2},{4,5},{5,4},{6,7},{7,6},{8,9},{9,8},{10,11... | collective-permute-start | bytes 6291464 | tf_op jit(solution)/shard_map/ppermute | solution.py:130
  5.6 6.8 %collective-permute-start.1 = (f32[32,128]{1,0:T(8,128)}, f32[32,128]{1,0:T(8,128)S(1)}, u32[]{:S(2)}, u32[]{:S(2)}) collective-permute-start(f32[32,128]{1,0:T(8,128)} %get-tuple-element.25), channel_id=1, source_target_pairs={{0,1},{1,0},{2,3},{3,2},{4,5},{5,4},{6,7},{7,6},{8,9},{9,8},{10,11... | collective-permute-start | bytes 49160 | tf_op jit(solution)/shard_map/ppermute | solution.py:130
  17.1 9.9 %collective-permute-start.2 = (f16[264,512]{1,0:T(8,128)(2,1)}, f16[264,512]{1,0:T(8,128)(2,1)S(1)}, u32[]{:S(2)}, u32[]{:S(2)}) collective-permute-start(f16[264,512]{1,0:T(8,128)(2,1)} %get-tuple-element.52), channel_id=1, source_target_pairs={{0,2},{2,4},{4,6},{6,0},{1,3},{3,5},{5,7},{7,1},{8,10},{10,12},{12... | collective-permute-start | bytes 811016 | tf_op jit(solution)/shard_map/ppermute | solution.py:126
  18.7 9.4 %collective-permute-start.4 = (f16[264,512]{1,0:T(8,128)(2,1)S(1)}, f16[264,512]{1,0:T(8,128)(2,1)S(1)}, u32[]{:S(2)}, u32[]{:S(2)}) collective-permute-start(f16[264,512]{1,0:T(8,128)(2,1)S(1)} %get-tuple-element.53), channel_id=1, source_target_pairs={{0,6},{2,0},{4,2},{6,4},{1,7},{3,1},{5,3},{7,5},{8,14},{10,8},{12,... | collective-permute-start | bytes 811016 | tf_op jit(solution)/shard_map/ppermute | solution.py:126
  20.4 13.6 %collective-permute-start.3 = (f16[264,512]{1,0:T(8,128)(2,1)S(1)}, f16[264,512]{1,0:T(8,128)(2,1)S(1)}, u32[]{:S(2)}, u32[]{:S(2)}) collective-permute-start(f16[264,512]{1,0:T(8,128)(2,1)S(1)} %get-tuple-element.54), channel_id=1, source_target_pairs={{0,4},{2,6},{4,0},{6,2},{1,5},{3,7},{5,1},{7,3},{8,12},{10,14},{12... | collective-permute-start | bytes 811016 | tf_op jit(solution)/shard_map/ppermute | solution.py:126
  35.6 9.4 %collective-permute-start.7 = (f16[264,512]{1,0:T(8,128)(2,1)S(1)}, f16[264,512]{1,0:T(8,128)(2,1)S(1)}, u32[]{:S(2)}, u32[]{:S(2)}) collective-permute-start(f16[264,512]{1,0:T(8,128)(2,1)S(1)} %pad_maximum_fusion.3), channel_id=1, source_target_pairs={{0,6},{2,0},{4,2},{6,4},{1,7},{3,1},{5,3},{7,5},{8,14},{10,8},{12,... | collective-permute-start | bytes 811016 | tf_op jit(solution)/shard_map/ppermute | solution.py:126
  37.3 10.9 %collective-permute-start.6 = (f16[264,512]{1,0:T(8,128)(2,1)S(1)}, f16[264,512]{1,0:T(8,128)(2,1)S(1)}, u32[]{:S(2)}, u32[]{:S(2)}) collective-permute-start(f16[264,512]{1,0:T(8,128)(2,1)S(1)} %pad_maximum_fusion.3), channel_id=1, source_target_pairs={{0,4},{2,6},{4,0},{6,2},{1,5},{3,7},{5,1},{7,3},{8,12},{10,14},{12... | collective-permute-start | bytes 811016 | tf_op jit(solution)/shard_map/ppermute | solution.py:126
  38.8 12.6 %collective-permute-start.5 = (f16[264,512]{1,0:T(8,128)(2,1)S(1)}, f16[264,512]{1,0:T(8,128)(2,1)S(1)}, u32[]{:S(2)}, u32[]{:S(2)}) collective-permute-start(f16[264,512]{1,0:T(8,128)(2,1)S(1)} %pad_maximum_fusion.3), channel_id=1, source_target_pairs={{0,2},{2,4},{4,6},{6,0},{1,3},{3,5},{5,7},{7,1},{8,10},{10,12},{12... | collective-permute-start | bytes 811016 | tf_op jit(solution)/shard_map/ppermute | solution.py:126
  52.9 1.4 %collective-permute-start.8 = (f32[64,512]{1,0:T(8,128)S(1)}, f32[64,512]{1,0:T(8,128)S(1)}, u32[]{:S(2)}, u32[]{:S(2)}) collective-permute-start(f32[64,512]{1,0:T(8,128)S(1)} %get-tuple-element.29), channel_id=1, source_target_pairs={{0,1},{1,0},{2,3},{3,2},{4,5},{5,4},{6,7},{7,6},{8,9},{9,8},{10,11... | collective-permute-start | bytes 393224 | tf_op jit(solution)/shard_map/ppermute | solution.py:130
  55.0 9.1 %collective-permute-start.9 = (bf16[1024,512]{1,0:T(8,128)(2,1)S(1)}, bf16[1024,512]{1,0:T(8,128)(2,1)S(1)}, u32[]{:S(2)}, u32[]{:S(2)}) collective-permute-start(bf16[1024,512]{1,0:T(8,128)(2,1)S(1)} %get-tuple-element.31.hm_ref.refs_8_), channel_id=1, source_target_pairs={{0,1},{1,0},{2,3},{3,2},{4,5},{5,4},{6,7},{7,6},{8,9},{9,8},{10,11... | collective-permute-start | bytes 3145736 | tf_op jit(solution)/shard_map/ppermute | solution.py:130
  55.1 8.9 %collective-permute-start.10 = (bf16[1024,512]{1,0:T(8,128)(2,1)S(1)}, bf16[1024,512]{1,0:T(8,128)(2,1)}, u32[]{:S(2)}, u32[]{:S(2)}) collective-permute-start(bf16[1024,512]{1,0:T(8,128)(2,1)S(1)} %get-tuple-element.32.lm_ref.refs_9_), channel_id=1, source_target_pairs={{0,1},{1,0},{2,3},{3,2},{4,5},{5,4},{6,7},{7,6},{8,9},{9,8},{10,11... | collective-permute-start | bytes 3145736 | tf_op jit(solution)/shard_map/ppermute | solution.py:130
  55.5 16.5 %all-to-all-start = ((f32[8,8,512]{2,1,0:T(8,128)}), f32[8,8,512]{2,1,0:T(8,128)S(1)}, u32[]{:S(2)}, u32[]{:S(2)}) async-start(f32[8,8,512]{2,1,0:T(8,128)} %bitcast.16), calls=%async_computation | async-start | bytes 262144 | tf_op jit(solution)/shard_map/all_to_all | solution.py:121
  72.0 5.0 %collective-permute-start.13 = (f32[8,512]{1,0:T(8,128)S(1)}, f32[8,512]{1,0:T(8,128)S(1)}, u32[]{:S(2)}, u32[]{:S(2)}) collective-permute-start(f32[8,512]{1,0:T(8,128)S(1)} %reduce_sum.9), channel_id=1, source_target_pairs={{0,192},{64,128},{128,64},{192,0},{1,193},{65,129},{129,65},{193,1... | collective-permute-start | bytes 49160 | tf_op jit(solution)/shard_map/ppermute | solution.py:130
  74.9 5.2 %collective-permute-start.12 = (f32[8,512]{1,0:T(8,128)S(1)}, f32[8,512]{1,0:T(8,128)S(1)}, u32[]{:S(2)}, u32[]{:S(2)}) collective-permute-start(f32[8,512]{1,0:T(8,128)S(1)} %reduce_sum.9), channel_id=1, source_target_pairs={{0,128},{64,192},{128,0},{192,64},{1,129},{65,193},{129,1},{193,65... | collective-permute-start | bytes 49160 | tf_op jit(solution)/shard_map/ppermute | solution.py:130
  75.7 4.5 %collective-permute-start.11 = (f32[8,512]{1,0:T(8,128)S(1)}, f32[8,512]{1,0:T(8,128)S(1)}, u32[]{:S(2)}, u32[]{:S(2)}) collective-permute-start(f32[8,512]{1,0:T(8,128)S(1)} %reduce_sum.9), channel_id=1, source_target_pairs={{0,64},{64,0},{128,192},{192,128},{1,65},{65,1},{129,193},{193,129... | collective-permute-start | bytes 49160 | tf_op jit(solution)/shard_map/ppermute | solution.py:130
  80.8 13.7 %all-to-all-start.1 = ((f32[8,8,512]{2,1,0:T(8,128)}), f32[8,8,512]{2,1,0:T(8,128)S(1)}, u32[]{:S(2)}, u32[]{:S(2)}) async-start(f32[8,8,512]{2,1,0:T(8,128)} %broadcast_in_dim.2), calls=%async_computation.1 | async-start | bytes 262144 | tf_op jit(solution)/shard_map/all_to_all | solution.py:121
  94.5 40.5 %all-to-all-start.2 = ((bf16[32,32,512]{2,1,0:T(8,128)(2,1)}), bf16[32,32,512]{2,1,0:T(8,128)(2,1)S(1)}, u32[]{:S(2)}, u32[]{:S(2)}) async-start(bf16[32,32,512]{2,1,0:T(8,128)(2,1)} %bitcast.32), calls=%async_computation.2 | async-start | bytes 2097152 | tf_op jit(solution)/shard_map/all_to_all | solution.py:121
  101.5 5.0 %collective-permute-start.16 = (f32[64,512]{1,0:T(8,128)S(1)}, f32[64,512]{1,0:T(8,128)S(1)}, u32[]{:S(2)}, u32[]{:S(2)}) collective-permute-start(f32[64,512]{1,0:T(8,128)S(1)} %bitcast.37), channel_id=1, source_target_pairs={{0,6},{2,0},{4,2},{6,4},{1,7},{3,1},{5,3},{7,5},{8,14},{10,8},{12,... | collective-permute-start | bytes 393224 | tf_op jit(solution)/shard_map/ppermute | solution.py:126
  102.2 6.5 %collective-permute-start.15 = (f32[64,512]{1,0:T(8,128)S(1)}, f32[64,512]{1,0:T(8,128)S(1)}, u32[]{:S(2)}, u32[]{:S(2)}) collective-permute-start(f32[64,512]{1,0:T(8,128)S(1)} %bitcast.38), channel_id=1, source_target_pairs={{0,4},{2,6},{4,0},{6,2},{1,5},{3,7},{5,1},{7,3},{8,12},{10,14},{12... | collective-permute-start | bytes 393224 | tf_op jit(solution)/shard_map/ppermute | solution.py:126
  103.8 6.2 %collective-permute-start.14 = (f32[64,512]{1,0:T(8,128)S(1)}, f32[64,512]{1,0:T(8,128)S(1)}, u32[]{:S(2)}, u32[]{:S(2)}) collective-permute-start(f32[64,512]{1,0:T(8,128)S(1)} %bitcast.39), channel_id=1, source_target_pairs={{0,2},{2,4},{4,6},{6,0},{1,3},{3,5},{5,7},{7,1},{8,10},{10,12},{12... | collective-permute-start | bytes 393224 | tf_op jit(solution)/shard_map/ppermute | solution.py:126
  104.7 5.4 %collective-permute-start.17 = (f32[64,512]{1,0:T(8,128)S(1)}, f32[64,512]{1,0:T(8,128)S(1)}, u32[]{:S(2)}, u32[]{:S(2)}) collective-permute-start(f32[64,512]{1,0:T(8,128)S(1)} %bitcast.40), channel_id=1, source_target_pairs={{0,1},{1,0},{2,3},{3,2},{4,5},{5,4},{6,7},{7,6},{8,9},{9,8},{10,11... | collective-permute-start | bytes 393224 | tf_op jit(solution)/shard_map/ppermute | solution.py:130
  106.6 3.5 %collective-permute-start.20 = (f32[64,512]{1,0:T(8,128)S(1)}, f32[64,512]{1,0:T(8,128)S(1)}, u32[]{:S(2)}, u32[]{:S(2)}) collective-permute-start(f32[64,512]{1,0:T(8,128)S(1)} %collective-permute-done.16.refs_3_), channel_id=1, source_target_pairs={{0,1},{1,0},{2,3},{3,2},{4,5},{5,4},{6,7},{7,6},{8,9},{9,8},{10,11... | collective-permute-start | bytes 393224 | tf_op jit(solution)/shard_map/ppermute | solution.py:130
  108.7 1.4 %collective-permute-start.19 = (f32[64,512]{1,0:T(8,128)S(1)}, f32[64,512]{1,0:T(8,128)S(1)}, u32[]{:S(2)}, u32[]{:S(2)}) collective-permute-start(f32[64,512]{1,0:T(8,128)S(1)} %collective-permute-done.15.refs_2_), channel_id=1, source_target_pairs={{0,1},{1,0},{2,3},{3,2},{4,5},{5,4},{6,7},{7,6},{8,9},{9,8},{10,11... | collective-permute-start | bytes 393224 | tf_op jit(solution)/shard_map/ppermute | solution.py:130
  110.1 1.3 collective-permute-start.18
  (13 other events, 70.6 us)
